TPU v7x, 128 devices: a whole 4x4x4 slice. The times are simulated.
128 devices in a mesh: grp: 8 (over z, y_hi), tm: 16 (over x, y_lo, core).
Axes of the slice: x: 4, y: 4 (y_hi: 2, y_lo: 2; y = y_hi * 2 + y_lo), z: 4, core: 2. Of those that a mesh axis runs over, the one named last changes fastest.
Arguments:
- initial: float32 [16, 16384], P('grp'), parts along dimension 0, may hold values from -1 to 1
- forcing: float32 [16, 64, 16384], P('grp', 'tm'), parts along dimension 0, may hold values from -1.8 to 1.8
- fine_blocks: float32 [16, 3, 128, 128], replicated, may hold values from -0.2 to 0.9, as said below
- coarse_blocks: float32 [16, 3, 128, 128], replicated, may hold values from -0.2 to 0.9, as said below
Outputs:
- solution: float32 [16, 64, 16384], P('grp', 'tm'), parts along dimension 0
There are 8 independent parts, one for each index of `grp`. A program takes and returns all parts, laid end to end along the dimension named above; an argument that names none is the same for every part. Nothing has to cross between parts.
Inputs may be any that keep to these rules, and one draw needn't show every extreme that they name: `fine_blocks`: 16 x 3 blocks of 128 x 128. `coarse_blocks`: 16 x 3 blocks of 128 x 128.
All inputs are finite; a program needn't handle non-finite values.
Results may differ from a plain program's by a relative error of at most 0.00013.
Values sent between devices are 32-bit elements; how exact they have to be, the bound alone decides.
No kernel may reach another device: no remote copies, remote signals or barrier semaphores. Data moves between devices by JAX's collectives and lax.ppermute only.
A program may use at most 64 MiB of HBM per device.

v0:
```python
import functools

import jax
import jax.numpy as jnp
from jax import lax
from jax.experimental import pallas as pl
from jax.experimental.pallas import tpu as pltpu
from jax.sharding import PartitionSpec as P


M = 4
DELTA = 0.05
BLK = 128
BF16 = jnp.bfloat16
F32 = jnp.float32


def split(value):
    high = value.astype(BF16)
    low = (value - high.astype(F32)).astype(BF16)
    return jnp.concatenate([high, low], axis=0)


def shifted(value, down):
    parts = []
    for part in jnp.split(value, value.shape[0] // 8, axis=0):
        rows = lax.broadcasted_iota(jnp.int32, part.shape, 0)
        moved = pltpu.roll(part, 1 if down else 7, axis=0)
        parts.append(jnp.where(rows == (0 if down else 7), 0.0, moved))
    return jnp.concatenate(parts, axis=0)


def put(state_ref, zone, value):
    zones = state_ref.shape[0] - 2
    state_ref[zone + 1] = split(value)
    if zone == zones - 1:
        state_ref[0] = split(shifted(value, True))
    if zone == 0:
        state_ref[zones + 1] = split(shifted(value, False))


def solve(mixing, step):
    solved = mixing
    for _ in range(2):
        squared = solved * solved
        solved = (mixing + (2.0 * step * solved) * squared) / ((1.0 - step) + (3.0 * step) * squared)
    return solved


def propagate_zone(state_ref, weights_ref, zone, step):
    rows = state_ref.shape[1] // 2
    product = sum(
        jnp.dot(state_ref[zone + k], weights_ref[zone, k * BLK:(k + 1) * BLK], preferred_element_type=F32)
        for k in range(3)
    )
    low, high = product[rows:], product[:rows]
    mixing = high[:, :BLK] + (high[:, BLK:] + (low[:, :BLK] + low[:, BLK:]))
    return solve(mixing, step)


def zone_order(zones, start):
    return [(start + i) % zones for i in range(zones)]


def prepare_zone(block_ref, out_ref, zone):
    for k in range(3):
        turned = block_ref[zone, k].T
        high = turned.astype(BF16)
        out_ref[zone, k * BLK:(k + 1) * BLK, :BLK] = high
        out_ref[zone, k * BLK:(k + 1) * BLK, BLK:] = (turned - high.astype(F32)).astype(BF16)


def fetches(blocks_ref, held_ref, sems):
    count = sems.shape[0]
    size = blocks_ref.shape[0] // count
    spans = [pl.ds(i * size, size) for i in range(count)]
    return [pltpu.make_async_copy(blocks_ref.at[s], held_ref.at[s], sems.at[i]) for i, s in enumerate(spans)]


def prepare_all(copies, held_ref, out_ref):
    size = held_ref.shape[0] // len(copies)
    for i, copy in enumerate(copies):
        copy.wait()
        for z in range(i * size, (i + 1) * size):
            prepare_zone(held_ref, out_ref, z)


def prepare_kernel(blocks_ref, out_ref):
    for z in range(blocks_ref.shape[0]):
        prepare_zone(blocks_ref, out_ref, z)


def place():
    index = lax.axis_index("tm")
    return index, index & 1, (index >> 1) & 1, index >> 2


VMEM = pl.BlockSpec(memory_space=pltpu.VMEM)


def force_rows(force_ref, zone, slot):
    per = force_ref.shape[0] // 2
    zones = per // (M * 8)
    return jnp.concatenate(
        [force_ref[pl.ds(i * per + zone * M + slot, 8, stride=zones * M), :] for i in range(2)], axis=0
    )


def first_rows(initial_ref, zone):
    zones = initial_ref.shape[0] // 16
    return jnp.concatenate([initial_ref[pl.ds(zone * 2 + i, 8, stride=zones * 2), :] for i in range(2)], axis=0)


def relax_kernel(start_ref, given_ref, blocks_ref, next_blocks_ref, out_ref, weights_ref, next_held_ref,
                 state_a, state_b, held_ref, sems, initial_ref, force_ref, early_sems, late_sems):
    zones = weights_ref.shape[0]
    leading = place()[0] == 0
    early = [
        pltpu.make_async_copy(given_ref, force_ref, early_sems.at[0]),
        pltpu.make_async_copy(start_ref, initial_ref, early_sems.at[1]),
    ]
    copies = fetches(blocks_ref, held_ref, sems)
    for copy in early + copies:
        copy.start()
    for copy in early:
        copy.wait()
    for z in range(zones):
        put(state_a, z, force_rows(force_ref, z, 0))
    prepare_all(copies, held_ref, weights_ref)
    late = fetches(next_blocks_ref, next_held_ref, late_sems)
    for copy in late:
        copy.start()

    @pl.when(leading)
    def _():
        for z in range(zones):
            put(state_b, z, first_rows(initial_ref, z))
        for z in range(zones):
            put(state_a, z, propagate_zone(state_b, weights_ref, z, DELTA) + force_rows(force_ref, z, 0))

    source, target = state_a, state_b
    for slot in range(1, M):
        for z in zone_order(zones, slot - 1):
            value = propagate_zone(source, weights_ref, z, DELTA) + force_rows(force_ref, z, slot)
            if slot < M - 1:
                put(target, z, value)
            else:
                out_ref[z] = value
        source, target = target, source
    for copy in late:
        copy.wait()


def residual_kernel(initial_ref, carried_ref, force_ref, fine_ref, coarse_ref, out_ref,
                    state_a, state_b, coarse_part):
    zones = fine_ref.shape[0]
    index = place()[0]
    for z in range(zones):
        put(state_a, z, jnp.where(index == 0, first_rows(initial_ref, z), carried_ref[z]))
    for z in range(zones):
        coarse_part[z] = jnp.where(index < 2, 0.0, propagate_zone(state_a, coarse_ref, z, DELTA * M))
    source, target = state_a, state_b
    for slot in range(M):
        for z in zone_order(zones, slot):
            value = propagate_zone(source, fine_ref, z, DELTA) + force_rows(force_ref, z, slot)
            if slot < M - 1:
                put(target, z, value)
            else:
                out_ref[z] = value - coarse_part[z]
        source, target = target, source


def march(source, target, coarse_ref, held_ref, rights, slot, done=None):
    zones = coarse_ref.shape[0]
    for step, right in enumerate(rights):
        for z in zone_order(zones, step):
            value = propagate_zone(source, coarse_ref, z, DELTA * M) + right(z)
            held_ref[slot + step + 1, z] = value
            if step < len(rights) - 1:
                put(target, z, value)
            elif done is not None:
                done[z] = value
        source, target = target, source


def first_chain_kernel(initial_ref, own_ref, before_ref, coarse_ref, near_ref, first_ref, held_ref, next_ref, state_a, state_b):
    zones = coarse_ref.shape[0]
    _, core, row, plane = place()

    @pl.when((plane == 0) & (core == 1) & (row == 0))
    def _():
        for z in range(zones):
            held_ref[0, z] = first_rows(initial_ref, z)
            held_ref[1, z] = before_ref[z]
            held_ref[2, z] = own_ref[z]

    @pl.when((plane == 0) & (core == 1) & (row == 1))
    def _():
        for z in range(zones):
            held_ref[2, z] = first_ref[z]
            put(state_a, z, first_ref[z])
        march(state_a, state_b, coarse_ref, held_ref, [lambda z: near_ref[z], lambda z: own_ref[z]], 2, next_ref)


def chain_kernel(turn, incoming_refs, own_ref, near_ref, coarse_ref, far_ref, side_ref, held_ref, next_ref,
                 state_a, state_b):
    zones = coarse_ref.shape[0]
    _, core, row, plane = place()
    upper = row == 0
    rights = [
        lambda z: jnp.where(upper, near_ref[z], far_ref[z]),
        lambda z: jnp.where(upper, own_ref[z], side_ref[z]),
        lambda z: jnp.where(upper, far_ref[z], near_ref[z]),
        lambda z: jnp.where(upper, side_ref[z], own_ref[z]),
    ]

    @pl.when((plane == turn) & (core == 1))
    def _():
        for z in range(zones):
            held_ref[0, z] = arrived(incoming_refs, upper, z)
            put(state_a, z, held_ref[0, z])
        march(state_a, state_b, coarse_ref, held_ref, rights, 0, next_ref)


def arrived(incoming_refs, upper, zone):
    if len(incoming_refs) == 1:
        return incoming_refs[0][zone]
    return jnp.where(upper, incoming_refs[0][zone], incoming_refs[1][zone])


def enter_kernel(turn, incoming_ref, far_ref, side_ref, coarse_ref, old_ref, held_ref, give_ref, state_a, state_b):
    del old_ref
    zones = coarse_ref.shape[0]
    _, core, row, plane = place()
    here = (plane == turn) & (core == 1)

    @pl.when(here & (row == 0))
    def _():
        held_ref[0] = incoming_ref[...]

    @pl.when(here & (row == 1))
    def _():
        for z in range(zones):
            put(state_a, z, incoming_ref[z])
        march(state_a, state_b, coarse_ref, held_ref, [lambda z: far_ref[z], lambda z: side_ref[z]], 0)

    give_ref[...] = held_ref[row * 2]


def leave_kernel(turn, own_ref, near_ref, coarse_ref, old_ref, held_ref, give_ref, state_a, state_b):
    zones = coarse_ref.shape[0]
    _, core, row, plane = place()

    @pl.when((plane == turn) & (core == 1))
    def _():
        for z in range(zones):
            put(state_a, z, old_ref[row * 2, z])
        march(state_a, state_b, coarse_ref, held_ref, [lambda z: near_ref[z], lambda z: own_ref[z]], row * 2)

    give_ref[...] = held_ref[row * 2 + 1]


def final_kernel(held_ref, swapped_ref, force_ref, fine_ref, out_ref, state_a, state_b):
    zones = fine_ref.shape[0]
    per = out_ref.shape[0] // 2
    _, core, row, _ = place()
    for z in range(zones):
        put(state_a, z, jnp.where(core == 1, held_ref[row * 2 + 1, z], swapped_ref[z]))
    source, target = state_a, state_b
    for step in range(M - 1):
        for z in zone_order(zones, step):
            value = propagate_zone(source, fine_ref, z, DELTA) + force_rows(force_ref, z, step)
            for i in range(2):
                out_ref[pl.ds(i * per + z * M + step, 8, stride=zones * M), :] = value[i * 8:(i + 1) * 8]
            if step < M - 2:
                put(target, z, value)
        source, target = target, source


def corners_kernel(steps_ref, held_ref, swapped_ref, out_ref):
    zones = swapped_ref.shape[0]
    per = out_ref.shape[0] // 2
    _, core, row, _ = place()
    out_ref[...] = steps_ref[...]
    for z in range(zones):
        value = jnp.where(core == 1, held_ref[row * 2 + 2, z], swapped_ref[z])
        for i in range(2):
            out_ref[pl.ds(i * per + z * M + M - 1, 8, stride=zones * M), :] = value[i * 8:(i + 1) * 8]


def states(zones, rows):
    return [pltpu.VMEM((zones + 2, 2 * rows, BLK), BF16)] * 2


HBM = pl.BlockSpec(memory_space=pltpu.HBM)


def call(kernel, in_specs, out_shape, scratch, mib, flops, aliases=None):
    return pl.pallas_call(
        kernel,
        in_specs=in_specs,
        out_specs=jax.tree.map(lambda _: VMEM, out_shape),
        out_shape=out_shape,
        scratch_shapes=scratch,
        input_output_aliases=aliases or {},
        compiler_params=pltpu.CompilerParams(vmem_limit_bytes=mib * 2**20),
        cost_estimate=pl.CostEstimate(flops=flops, bytes_accessed=10**6, transcendentals=0),
    )


def body(initial, forcing, fine_blocks, coarse_blocks):
    members, times, cells = forcing.shape
    blocks = cells // BLK
    zones = fine_blocks.shape[0]
    depth = blocks // zones
    rows = members * depth
    count = lax.axis_size("tm")

    force = forcing.reshape(members, times, blocks, BLK).transpose(0, 2, 1, 3).reshape(members * blocks * times, BLK)
    start = initial.reshape(members, blocks, BLK).transpose(1, 0, 2).reshape(blocks * members, BLK)
    fine_blocks = pltpu.with_memory_space_constraint(fine_blocks, pltpu.HBM)
    coarse_blocks = pltpu.with_memory_space_constraint(coarse_blocks, pltpu.HBM)
    weights = jax.ShapeDtypeStruct((zones, 3 * BLK, 2 * BLK), BF16)
    full = jax.ShapeDtypeStruct((zones, rows, BLK), F32)
    held_states = jax.ShapeDtypeStruct((M + 1, zones, rows, BLK), F32)
    held = [pltpu.VMEM(fine_blocks.shape, F32), pltpu.SemaphoreType.DMA((4,))]

    def sent(value, even, odd):
        return lax.ppermute(value, "tm", [(i, (odd if i % 2 else even)(i) % count) for i in range(count)])

    early = [pltpu.VMEM(start.shape, F32), pltpu.VMEM(force.shape, F32), pltpu.SemaphoreType.DMA((2,))]
    late = [pltpu.SemaphoreType.DMA((4,))]
    corner, fine, coarse_blocks = call(
        relax_kernel, [HBM] * 4, [full, weights, jax.ShapeDtypeStruct(coarse_blocks.shape, F32)],
        states(zones, rows) + held + early + late, 20, 10**9,
    )(pltpu.with_memory_space_constraint(start, pltpu.HBM), pltpu.with_memory_space_constraint(force, pltpu.HBM),
      fine_blocks, coarse_blocks)
    carried = sent(corner, lambda i: i + 1, lambda i: i + 1)
    coarse = call(prepare_kernel, [VMEM], weights, [], 8, 10**9)(coarse_blocks)
    right = call(
        residual_kernel, [VMEM] * 5, full,
        states(zones, rows) + [pltpu.VMEM((zones, rows, BLK), F32)], 14, 10**9,
    )(start, carried, force, fine, coarse)

    def relayed(value, moves):
        target = {i: i ^ 1 for i in range(count)}
        for a, b in moves:
            target.update({2 * a + 1: 2 * b + 1, 2 * b + 1: 2 * b, 2 * b: 2 * a, 2 * a: 2 * a + 1})
        return lax.ppermute(value, "tm", list(target.items()))

    urgent = {i: i ^ 1 for i in range(count)}
    urgent.update({1: 3, 3: 2, 2: 1, 0: count - 4, count - 4: count - 3, count - 3: 0})
    first = lax.ppermute(right, "tm", list(urgent.items()))
    near = sent(right, lambda i: i ^ 1, lambda i: i ^ 1)
    far = sent(right, lambda i: i ^ 3, lambda i: i ^ 1)

    def chain(kernel, inputs, outputs, held=None):
        return call(
            kernel, [VMEM] * (len(inputs) + (held is not None)), [held_states] + [full] * outputs,
            states(zones, rows), 10, 10**9, None if held is None else {len(inputs): 0},
        )(*inputs, *(() if held is None else (held,)))

    def middle(turn, arrivals):
        def kernel(*refs):
            incoming_refs, rest = refs[5:5 + arrivals], refs[:5] + refs[6 + arrivals:]
            chain_kernel(turn, incoming_refs, *rest)

        return kernel

    held, following = chain(first_chain_kernel, (start, right, carried, coarse, near, first), 1)
    behind, following = lax.optimization_barrier((right, following))
    side = sent(behind, lambda i: i ^ 2, lambda i: i ^ 2)
    across = relayed(following, [(1, 2)])
    along = relayed(following, [(1, 3)])
    incoming = (across, along)
    last = count // 4 - 1
    for turn in range(1, last):
        held, following = chain(
            middle(turn, len(incoming)), (right, near, coarse, far, side, *incoming), 1, held)
        incoming = (relayed(following, [(2 * turn + y, 2 * turn + 2 + y) for y in range(2)]),)
    held, give = chain(
        functools.partial(enter_kernel, last), (*incoming, far, side, coarse), 1, held)
    swapped = sent(give, lambda i: i ^ 1, lambda i: i ^ 1)
    held, give = chain(functools.partial(leave_kernel, last), (right, near, coarse), 1, held)
    corners = sent(give, lambda i: i ^ 1, lambda i: i ^ 1)
    forces = jax.ShapeDtypeStruct(force.shape, F32)
    steps = call(final_kernel, [VMEM] * 4, forces, states(zones, rows), 10, 10**9)(held, swapped, force, fine)
    result = call(corners_kernel, [VMEM] * 3, forces, [], 6, 10**6)(steps, held, corners)
    return result.reshape(members, blocks, times, BLK).transpose(0, 2, 1, 3).reshape(members, times, cells)


def solution(mesh):
    in_specs = (P("grp", None), P("grp", "tm", None), P(), P())
    out_specs = P("grp", "tm", None)
    return jax.shard_map(body, mesh=mesh, in_specs=in_specs, out_specs=out_specs, check_vma=False)
```

profile of v0, /device:TPU:63, one launch (start us, length us, event | category | flops | bytes accessed | tf_op | source)
XLA Modules:
  0.0 36.6 jit_solution(17685353582438324438)
XLA Ops:
  0.0 4.6 %shard_map.46 = (f32[16,16,128]{2,1,0:T(8,128)S(1)}, bf16[16,384,256]{2,1,0:T(8,128)(2,1)S(1)}, f32[16,3,128,128]{3,2,1,0:T(8,128)S(1)}) custom-call(f32[256,128]{1,0:T(8,128)} %bitcast.18, f32[1024,128]{1,0:T(8,128)} %bitcast.15, f32[16,3,128,128]{3,2,1,0:T(8,128)} %blocks_ref.1, f32[16,3,128,128]{3,2,1,0:T(8,128)} %next_blocks_ref.1), custom_call_target="tpu_custom_call" | custom-call | flops 1000000000 | bytes 1000000 | tf_op jit(solution)/shard_map/pallas_call | solution.py:333
  4.6 1.4 %collective-permute-start = (f32[16,16,128]{2,1,0:T(8,128)S(1)}, f32[16,16,128]{2,1,0:T(8,128)S(1)}, u32[]{:S(2)}, u32[]{:S(2)}) collective-permute-start(f32[16,16,128]{2,1,0:T(8,128)S(1)} %get-tuple-element.20), channel_id=1, source_target_pairs={{0,1},{1,2},{2,3},{3,4},{4,5},{5,6},{6,7},{7,8},{8,9},{9,10},{10,1... | collective-permute-start | bytes 393224 | tf_op jit(solution)/shard_map/ppermute | solution.py:329
  6.1 0.0 copy-start
  6.1 0.0 copy-start.1
  6.1 0.9 %shard_map.47.coarse_ref.refs_2_ = bf16[16,384,256]{2,1,0:T(8,128)(2,1)S(1)} custom-call(f32[16,3,128,128]{3,2,1,0:T(8,128)S(1)} %get-tuple-element.22.blocks_ref), custom_call_target="tpu_custom_call" | custom-call | flops 1000000000 | bytes 1000000 | tf_op jit(solution)/shard_map/pallas_call | solution.py:339
  7.0 1.1 %collective-permute-done.carried_ref.before_ref = f32[16,16,128]{2,1,0:T(8,128)S(1)} collective-permute-done((f32[16,16,128]{2,1,0:T(8,128)S(1)}, f32[16,16,128]{2,1,0:T(8,128)S(1)}, u32[]{:S(2)}, u32[]{:S(2)}) %collective-permute-start) | collective-permute-done | bytes 131104 | tf_op jit(solution)/shard_map/ppermute | solution.py:329
  8.0 0.0 copy-done
  8.0 0.0 copy-done.1
  8.0 2.2 %shard_map.48.own_ref.refs_0_ = f32[16,16,128]{2,1,0:T(8,128)S(1)} custom-call(f32[256,128]{1,0:T(8,128)S(1)} %bitcast.19, f32[16,16,128]{2,1,0:T(8,128)S(1)} %collective-permute-done.carried_ref.before_ref, f32[1024,128]{1,0:T(8,128)S(1)} %bitcast.16, bf16[16,384,256]{2,1,0:T(8,128)(2,1)S(1)} %get-tuple-element.21.fine_ref, ...), custom_call_target="tpu_custom_call" | custom-call | flops 1000000000 | bytes 1000000 | tf_op jit(solution)/shard_map/pallas_call | solution.py:340
  10.3 1.8 %collective-permute-start.3 = (f32[16,16,128]{2,1,0:T(8,128)S(1)}, f32[16,16,128]{2,1,0:T(8,128)S(1)}, u32[]{:S(2)}, u32[]{:S(2)}) collective-permute-start(f32[16,16,128]{2,1,0:T(8,128)S(1)} %shard_map.48.own_ref.refs_0_), channel_id=1, source_target_pairs={{0,12},{1,3},{2,1},{3,2},{4,5},{5,4},{6,7},{7,6},{8,9},{9,8},{10,1... | collective-permute-start | bytes 393224 | tf_op jit(solution)/shard_map/ppermute | solution.py:353
  12.1 0.1 collective-permute-start.1
  12.2 0.4 %collective-permute-start.2 = (f32[16,16,128]{2,1,0:T(8,128)S(1)}, f32[16,16,128]{2,1,0:T(8,128)S(1)}, u32[]{:S(2)}, u32[]{:S(2)}) collective-permute-start(f32[16,16,128]{2,1,0:T(8,128)S(1)} %shard_map.48.own_ref.refs_0_), channel_id=1, source_target_pairs={{0,3},{1,0},{2,1},{3,2},{4,7},{5,4},{6,5},{7,6},{8,11},{9,8},{10,9... | collective-permute-start | bytes 393224 | tf_op jit(solution)/shard_map/ppermute | solution.py:329
  12.6 0.5 %collective-permute-done.3.first_ref = f32[16,16,128]{2,1,0:T(8,128)S(1)} collective-permute-done((f32[16,16,128]{2,1,0:T(8,128)S(1)}, f32[16,16,128]{2,1,0:T(8,128)S(1)}, u32[]{:S(2)}, u32[]{:S(2)}) %collective-permute-start.3) | collective-permute-done | bytes 131104 | tf_op jit(solution)/shard_map/ppermute | solution.py:353
  13.1 0.4 collective-permute-done.1.near_ref.refs_1_
  13.4 3.7 %collective-permute-start.4 = (f32[16,16,128]{2,1,0:T(8,128)S(1)}, f32[16,16,128]{2,1,0:T(8,128)S(1)}, u32[]{:S(2)}, u32[]{:S(2)}) collective-permute-start(f32[16,16,128]{2,1,0:T(8,128)S(1)} %shard_map.48.own_ref.refs_0_), channel_id=1, source_target_pairs={{0,2},{1,3},{2,0},{3,1},{4,6},{5,7},{6,4},{7,5},{8,10},{9,11},{10,... | collective-permute-start | bytes 393224 | tf_op jit(solution)/shard_map/ppermute | solution.py:329
  17.1 2.8 %collective-permute-start.6 = (f32[16,16,128]{2,1,0:T(8,128)S(1)}, f32[16,16,128]{2,1,0:T(8,128)S(1)}, u32[]{:S(2)}, u32[]{:S(2)}) collective-permute-start(f32[16,16,128]{2,1,0:T(8,128)S(1)} %get-tuple-element.25), channel_id=1, source_target_pairs={{0,1},{1,0},{2,3},{3,7},{4,5},{5,4},{6,2},{7,6},{8,9},{9,8},{10,11... | collective-permute-start | bytes 393224 | tf_op jit(solution)/shard_map/ppermute | solution.py:349
  19.9 0.0 collective-permute-start.5
  19.9 0.0 collective-permute-done.2.refs_3_.far_ref
  19.9 0.0 collective-permute-done.4.refs_4_.side_ref
  19.9 1.0 %collective-permute-done.6.refs_6_ = f32[16,16,128]{2,1,0:T(8,128)S(1)} collective-permute-done((f32[16,16,128]{2,1,0:T(8,128)S(1)}, f32[16,16,128]{2,1,0:T(8,128)S(1)}, u32[]{:S(2)}, u32[]{:S(2)}) %collective-permute-start.6) | collective-permute-done | bytes 131104 | tf_op jit(solution)/shard_map/ppermute | solution.py:349
  20.9 0.4 collective-permute-done.5.refs_5_
  21.2 1.7 %collective-permute-start.7 = (f32[16,16,128]{2,1,0:T(8,128)S(1)}, f32[16,16,128]{2,1,0:T(8,128)S(1)}, u32[]{:S(2)}, u32[]{:S(2)}) collective-permute-start(f32[16,16,128]{2,1,0:T(8,128)S(1)} %get-tuple-element.27), channel_id=1, source_target_pairs={{0,1},{1,0},{2,3},{3,2},{4,5},{5,9},{6,7},{7,11},{8,4},{9,8},{10,6... | collective-permute-start | bytes 393224 | tf_op jit(solution)/shard_map/ppermute | solution.py:349
  22.9 1.0 %collective-permute-done.7.refs_5_ = f32[16,16,128]{2,1,0:T(8,128)S(1)} collective-permute-done((f32[16,16,128]{2,1,0:T(8,128)S(1)}, f32[16,16,128]{2,1,0:T(8,128)S(1)}, u32[]{:S(2)}, u32[]{:S(2)}) %collective-permute-start.7) | collective-permute-done | bytes 131104 | tf_op jit(solution)/shard_map/ppermute | solution.py:349
  23.9 0.4 collective-permute-start.8
  24.3 7.5 %collective-permute-done.8.incoming_ref = f32[16,16,128]{2,1,0:T(8,128)S(1)} collective-permute-done((f32[16,16,128]{2,1,0:T(8,128)S(1)}, f32[16,16,128]{2,1,0:T(8,128)S(1)}, u32[]{:S(2)}, u32[]{:S(2)}) %collective-permute-start.8) | collective-permute-done | bytes 131104 | tf_op jit(solution)/shard_map/ppermute | solution.py:349
  31.8 1.0 %shard_map.52 = (f32[5,16,16,128]{3,2,1,0:T(8,128)S(1)}, f32[16,16,128]{2,1,0:T(8,128)S(1)}) custom-call(f32[16,16,128]{2,1,0:T(8,128)S(1)} %collective-permute-done.8.incoming_ref, f32[16,16,128]{2,1,0:T(8,128)S(1)} %collective-permute-done.2.refs_3_.far_ref, ...), custom_call_target="tpu_custom_call", output_to_operand_aliasing={{0}: (4, {})} | custom-call | flops 1000000000 | bytes 1000000 | tf_op jit(solution)/shard_map/pallas_call | solution.py:358
  32.8 0.1 collective-permute-start.9
  32.9 1.0 %shard_map.53 = (f32[5,16,16,128]{3,2,1,0:T(8,128)S(1)}, f32[16,16,128]{2,1,0:T(8,128)S(1)}) custom-call(f32[16,16,128]{2,1,0:T(8,128)S(1)} %shard_map.48.own_ref.refs_0_, f32[16,16,128]{2,1,0:T(8,128)S(1)} %collective-permute-done.1.near_ref.refs_1_, bf16[16,384,256]{2,1,0:T(8,128)(2,1)S(1)} %shard_map.47.coarse_ref.refs_2_, ...), custom_call_target="tpu_custom_call", output_to_operand_aliasing={{0}: (3, {})} | custom-call | flops 1000000000 | bytes 1000000 | tf_op jit(solution)/shard_map/pallas_call | solution.py:358
  33.9 0.1 collective-permute-start.10
  34.0 0.2 collective-permute-done.9.swapped_ref
  34.2 1.4 %shard_map.54.steps_ref = f32[1024,128]{1,0:T(8,128)S(1)} custom-call(f32[5,16,16,128]{3,2,1,0:T(8,128)S(1)} %get-tuple-element.32.held_ref, f32[16,16,128]{2,1,0:T(8,128)S(1)} %collective-permute-done.9.swapped_ref, f32[1024,128]{1,0:T(8,128)S(1)} %bitcast.17, bf16[16,384,256]{2,1,0:T(8,128)(2,1)S(1)} %get-tuple-element.21.fine_ref), custom_call_target="tpu_custom_call" | custom-call | flops 1000000000 | bytes 1000000 | tf_op jit(solution)/shard_map/pallas_call | solution.py:387
  35.6 0.0 collective-permute-done.10.swapped_ref
  35.6 0.9 %shard_map.55 = f32[1024,128]{1,0:T(8,128)} custom-call(f32[1024,128]{1,0:T(8,128)S(1)} %shard_map.54.steps_ref, f32[5,16,16,128]{3,2,1,0:T(8,128)S(1)} %get-tuple-element.32.held_ref, f32[16,16,128]{2,1,0:T(8,128)S(1)} %collective-permute-done.10.swapped_ref), custom_call_target="tpu_custom_call" | custom-call | flops 1000000 | bytes 1000000 | tf_op jit(solution)/shard_map/pallas_call | solution.py:388
  (3 shorter events, 0.0 us)
Async XLA Ops:
  4.6 3.4 %collective-permute-start = (f32[16,16,128]{2,1,0:T(8,128)S(1)}, f32[16,16,128]{2,1,0:T(8,128)S(1)}, u32[]{:S(2)}, u32[]{:S(2)}) collective-permute-start(f32[16,16,128]{2,1,0:T(8,128)S(1)} %get-tuple-element.20), channel_id=1, source_target_pairs={{0,1},{1,2},{2,3},{3,4},{4,5},{5,6},{6,7},{7,8},{8,9},{9,10},{10,1... | collective-permute-start | bytes 393224 | tf_op jit(solution)/shard_map/ppermute | solution.py:329
  6.1 2.0 %copy-start = (f32[2,4,16384]{2,1,0:T(4,128)S(1)}, f32[2,4,16384]{2,1,0:T(4,128)}, u32[]{:S(2)}) copy-start(f32[2,4,16384]{2,1,0:T(4,128)} %param.5) | copy-start | bytes 1572868
  6.1 2.0 %copy-start.1 = (f32[2,16384]{1,0:T(2,128)S(1)}, f32[2,16384]{1,0:T(2,128)}, u32[]{:S(2)}) copy-start(f32[2,16384]{1,0:T(2,128)} %param.4) | copy-start | bytes 393220
  10.3 2.8 %collective-permute-start.3 = (f32[16,16,128]{2,1,0:T(8,128)S(1)}, f32[16,16,128]{2,1,0:T(8,128)S(1)}, u32[]{:S(2)}, u32[]{:S(2)}) collective-permute-start(f32[16,16,128]{2,1,0:T(8,128)S(1)} %shard_map.48.own_ref.refs_0_), channel_id=1, source_target_pairs={{0,12},{1,3},{2,1},{3,2},{4,5},{5,4},{6,7},{7,6},{8,9},{9,8},{10,1... | collective-permute-start | bytes 393224 | tf_op jit(solution)/shard_map/ppermute | solution.py:353
  12.1 1.3 %collective-permute-start.1 = (f32[16,16,128]{2,1,0:T(8,128)S(1)}, f32[16,16,128]{2,1,0:T(8,128)S(1)}, u32[]{:S(2)}, u32[]{:S(2)}) collective-permute-start(f32[16,16,128]{2,1,0:T(8,128)S(1)} %shard_map.48.own_ref.refs_0_), channel_id=1, source_target_pairs={{0,1},{1,0},{2,3},{3,2},{4,5},{5,4},{6,7},{7,6},{8,9},{9,8},{10,11... | collective-permute-start | bytes 393224 | tf_op jit(solution)/shard_map/ppermute | solution.py:329
  12.2 7.7 %collective-permute-start.2 = (f32[16,16,128]{2,1,0:T(8,128)S(1)}, f32[16,16,128]{2,1,0:T(8,128)S(1)}, u32[]{:S(2)}, u32[]{:S(2)}) collective-permute-start(f32[16,16,128]{2,1,0:T(8,128)S(1)} %shard_map.48.own_ref.refs_0_), channel_id=1, source_target_pairs={{0,3},{1,0},{2,1},{3,2},{4,7},{5,4},{6,5},{7,6},{8,11},{9,8},{10,9... | collective-permute-start | bytes 393224 | tf_op jit(solution)/shard_map/ppermute | solution.py:329
  13.4 6.5 %collective-permute-start.4 = (f32[16,16,128]{2,1,0:T(8,128)S(1)}, f32[16,16,128]{2,1,0:T(8,128)S(1)}, u32[]{:S(2)}, u32[]{:S(2)}) collective-permute-start(f32[16,16,128]{2,1,0:T(8,128)S(1)} %shard_map.48.own_ref.refs_0_), channel_id=1, source_target_pairs={{0,2},{1,3},{2,0},{3,1},{4,6},{5,7},{6,4},{7,5},{8,10},{9,11},{10,... | collective-permute-start | bytes 393224 | tf_op jit(solution)/shard_map/ppermute | solution.py:329
  17.1 3.8 %collective-permute-start.6 = (f32[16,16,128]{2,1,0:T(8,128)S(1)}, f32[16,16,128]{2,1,0:T(8,128)S(1)}, u32[]{:S(2)}, u32[]{:S(2)}) collective-permute-start(f32[16,16,128]{2,1,0:T(8,128)S(1)} %get-tuple-element.25), channel_id=1, source_target_pairs={{0,1},{1,0},{2,3},{3,7},{4,5},{5,4},{6,2},{7,6},{8,9},{9,8},{10,11... | collective-permute-start | bytes 393224 | tf_op jit(solution)/shard_map/ppermute | solution.py:349
  19.9 1.3 %collective-permute-start.5 = (f32[16,16,128]{2,1,0:T(8,128)S(1)}, f32[16,16,128]{2,1,0:T(8,128)S(1)}, u32[]{:S(2)}, u32[]{:S(2)}) collective-permute-start(f32[16,16,128]{2,1,0:T(8,128)S(1)} %get-tuple-element.25), channel_id=1, source_target_pairs={{0,1},{1,0},{2,3},{3,5},{4,2},{5,4},{6,7},{7,6},{8,9},{9,8},{10,11... | collective-permute-start | bytes 393224 | tf_op jit(solution)/shard_map/ppermute | solution.py:349
  21.2 2.7 %collective-permute-start.7 = (f32[16,16,128]{2,1,0:T(8,128)S(1)}, f32[16,16,128]{2,1,0:T(8,128)S(1)}, u32[]{:S(2)}, u32[]{:S(2)}) collective-permute-start(f32[16,16,128]{2,1,0:T(8,128)S(1)} %get-tuple-element.27), channel_id=1, source_target_pairs={{0,1},{1,0},{2,3},{3,2},{4,5},{5,9},{6,7},{7,11},{8,4},{9,8},{10,6... | collective-permute-start | bytes 393224 | tf_op jit(solution)/shard_map/ppermute | solution.py:349
  23.9 7.9 %collective-permute-start.8 = (f32[16,16,128]{2,1,0:T(8,128)S(1)}, f32[16,16,128]{2,1,0:T(8,128)S(1)}, u32[]{:S(2)}, u32[]{:S(2)}) collective-permute-start(f32[16,16,128]{2,1,0:T(8,128)S(1)} %get-tuple-element.29), channel_id=1, source_target_pairs={{0,1},{1,0},{2,3},{3,2},{4,5},{5,4},{6,7},{7,6},{8,9},{9,13},{10,1... | collective-permute-start | bytes 393224 | tf_op jit(solution)/shard_map/ppermute | solution.py:349
  32.8 1.4 %collective-permute-start.9 = (f32[16,16,128]{2,1,0:T(8,128)S(1)}, f32[16,16,128]{2,1,0:T(8,128)S(1)}, u32[]{:S(2)}, u32[]{:S(2)}) collective-permute-start(f32[16,16,128]{2,1,0:T(8,128)S(1)} %get-tuple-element.33), channel_id=1, source_target_pairs={{0,1},{1,0},{2,3},{3,2},{4,5},{5,4},{6,7},{7,6},{8,9},{9,8},{10,11... | collective-permute-start | bytes 393224 | tf_op jit(solution)/shard_map/ppermute | solution.py:329
  33.9 1.8 %collective-permute-start.10 = (f32[16,16,128]{2,1,0:T(8,128)S(1)}, f32[16,16,128]{2,1,0:T(8,128)S(1)}, u32[]{:S(2)}, u32[]{:S(2)}) collective-permute-start(f32[16,16,128]{2,1,0:T(8,128)S(1)} %get-tuple-element.34), channel_id=1, source_target_pairs={{0,1},{1,0},{2,3},{3,2},{4,5},{5,4},{6,7},{7,6},{8,9},{9,8},{10,11... | collective-permute-start | bytes 393224 | tf_op jit(solution)/shard_map/ppermute | solution.py:329
where the time goes:
time: 36.7 us; the launch traced here: 36.6 us
  starting transfers between devices  12.4 us (34%)
  Pallas kernels  12.1 us (33%)
  waiting for transfers between devices  12 us (33%)
    ppermute x4, waiting for transfers between devices, relayed(): return lax.ppermute(value, 'tm', list(target.items()))  9.82 us
    ppermute x6, starting transfers between devices, sent(): lax.ppermute(value, 'tm', [(i, (odd if i % 2 else even)(i) % count) for i...  5.82 us
    ppermute x4, starting transfers between devices, relayed(): return lax.ppermute(value, 'tm', list(target.items()))  4.81 us
    pallas_call x1, Pallas kernels, body(): call(relax_kernel, [HBM] * 4, [full, weights, jax.ShapeDtypeStruct(coarse...  4.61 us
    pallas_call x1, Pallas kernels, body(): call(residual_kernel, [VMEM] * 5, full, states(zones, rows) + [pltpu.VMEM...  2.23 us
    pallas_call x5, Pallas kernels, chain(): call(kernel, [VMEM] * (len(inputs) + (held is not None)), [held_states] +...  1.99 us
    ppermute x1, starting transfers between devices, body(): first = lax.ppermute(right, 'tm', list(urgent.items()))  1.81 us
    ppermute x6, waiting for transfers between devices, sent(): lax.ppermute(value, 'tm', [(i, (odd if i % 2 else even)(i) % count) for i...  1.66 us
  transfers between devices with their start and end apart: 11, of which 8 were waited for; matrix products, arithmetic and copies ran while one was open for 0% of the time, Pallas kernels for 9%

commit v1 on v0

--- a/solution.py
+++ b/solution.py
@@ -370,8 +370,14 @@
     held, following = chain(first_chain_kernel, (start, right, carried, coarse, near, first), 1)
     behind, following = lax.optimization_barrier((right, following))
     side = sent(behind, lambda i: i ^ 2, lambda i: i ^ 2)
-    across = relayed(following, [(1, 2)])
-    along = relayed(following, [(1, 3)])
+
+    def entered(chip):
+        target = {i: i ^ 1 for i in range(count)}
+        target.update({3: 2 * chip + 1, 2 * chip + 1: 2 * chip, 2 * chip: 3, 2: 0, 0: 1, 1: 2})
+        return lax.ppermute(following, "tm", list(target.items()))
+
+    across = entered(2)
+    along = entered(3)
     incoming = (across, along)
     last = count // 4 - 1
     for turn in range(1, last):

time: 36.7 us -> 35.3 us (0.962)
  the two profiles are of different devices: /device:TPU:63 before, /device:TPU:71 now
where the time goes in v1:
time: 35.3 us; the launch traced here: 35.2 us
  starting transfers between devices  13.2 us (37%)
  Pallas kernels  11.1 us (31%)
  waiting for transfers between devices  10.8 us (31%)
    ppermute x2, waiting for transfers between devices, relayed(): return lax.ppermute(value, 'tm', list(target.items()))  6.81 us
    pallas_call x1, Pallas kernels, body(): call(relax_kernel, [HBM] * 4, [full, weights, jax.ShapeDtypeStruct(coarse...  4.61 us
    ppermute x2, starting transfers between devices, relayed(): return lax.ppermute(value, 'tm', list(target.items()))  3.99 us
    ppermute x1, starting transfers between devices, body(): first = lax.ppermute(right, 'tm', list(urgent.items()))  3.96 us
    ppermute x2, starting transfers between devices, entered(): return lax.ppermute(following, 'tm', list(target.items()))  2.65 us
    ppermute x6, starting transfers between devices, sent(): lax.ppermute(value, 'tm', [(i, (odd if i % 2 else even)(i) % count) for i...  2.61 us
    ppermute x6, waiting for transfers between devices, sent(): lax.ppermute(value, 'tm', [(i, (odd if i % 2 else even)(i) % count) for i...  2.49 us
    pallas_call x1, Pallas kernels, body(): call(residual_kernel, [VMEM] * 5, full, states(zones, rows) + [pltpu.VMEM...  2.23 us
  transfers between devices with their start and end apart: 11, of which 7 were waited for; matrix products, arithmetic and copies ran while one was open for 0% of the time, Pallas kernels for 9%

profile of v1, /device:TPU:71, one launch (start us, length us, event | category | flops | bytes accessed | tf_op | source)
XLA Modules:
  0.0 35.2 jit_solution(11479274724105933537)
XLA Ops:
  0.0 4.6 %shard_map.46 = (f32[16,16,128]{2,1,0:T(8,128)S(1)}, bf16[16,384,256]{2,1,0:T(8,128)(2,1)S(1)}, f32[16,3,128,128]{3,2,1,0:T(8,128)S(1)}) custom-call(f32[256,128]{1,0:T(8,128)} %bitcast.18, f32[1024,128]{1,0:T(8,128)} %bitcast.15, f32[16,3,128,128]{3,2,1,0:T(8,128)} %blocks_ref.1, f32[16,3,128,128]{3,2,1,0:T(8,128)} %next_blocks_ref.1), custom_call_target="tpu_custom_call" | custom-call | flops 1000000000 | bytes 1000000 | tf_op jit(solution)/shard_map/pallas_call | solution.py:333
  4.6 1.9 %collective-permute-start = (f32[16,16,128]{2,1,0:T(8,128)S(1)}, f32[16,16,128]{2,1,0:T(8,128)S(1)}, u32[]{:S(2)}, u32[]{:S(2)}) collective-permute-start(f32[16,16,128]{2,1,0:T(8,128)S(1)} %get-tuple-element.20), channel_id=1, source_target_pairs={{0,1},{1,2},{2,3},{3,4},{4,5},{5,6},{6,7},{7,8},{8,9},{9,10},{10,1... | collective-permute-start | bytes 393224 | tf_op jit(solution)/shard_map/ppermute | solution.py:329
  6.5 0.0 copy-start
  6.5 0.0 copy-start.1
  6.6 0.9 %shard_map.47.coarse_ref.refs_2_ = bf16[16,384,256]{2,1,0:T(8,128)(2,1)S(1)} custom-call(f32[16,3,128,128]{3,2,1,0:T(8,128)S(1)} %get-tuple-element.22.blocks_ref), custom_call_target="tpu_custom_call" | custom-call | flops 1000000000 | bytes 1000000 | tf_op jit(solution)/shard_map/pallas_call | solution.py:339
  7.4 1.1 %collective-permute-done.carried_ref.before_ref = f32[16,16,128]{2,1,0:T(8,128)S(1)} collective-permute-done((f32[16,16,128]{2,1,0:T(8,128)S(1)}, f32[16,16,128]{2,1,0:T(8,128)S(1)}, u32[]{:S(2)}, u32[]{:S(2)}) %collective-permute-start) | collective-permute-done | bytes 131104 | tf_op jit(solution)/shard_map/ppermute | solution.py:329
  8.5 0.0 copy-done
  8.5 0.0 copy-done.1
  8.5 2.2 %shard_map.48.own_ref.refs_0_ = f32[16,16,128]{2,1,0:T(8,128)S(1)} custom-call(f32[256,128]{1,0:T(8,128)S(1)} %bitcast.19, f32[16,16,128]{2,1,0:T(8,128)S(1)} %collective-permute-done.carried_ref.before_ref, f32[1024,128]{1,0:T(8,128)S(1)} %bitcast.16, bf16[16,384,256]{2,1,0:T(8,128)(2,1)S(1)} %get-tuple-element.21.fine_ref, ...), custom_call_target="tpu_custom_call" | custom-call | flops 1000000000 | bytes 1000000 | tf_op jit(solution)/shard_map/pallas_call | solution.py:340
  10.7 4.0 %collective-permute-start.3 = (f32[16,16,128]{2,1,0:T(8,128)S(1)}, f32[16,16,128]{2,1,0:T(8,128)S(1)}, u32[]{:S(2)}, u32[]{:S(2)}) collective-permute-start(f32[16,16,128]{2,1,0:T(8,128)S(1)} %shard_map.48.own_ref.refs_0_), channel_id=1, source_target_pairs={{0,12},{1,3},{2,1},{3,2},{4,5},{5,4},{6,7},{7,6},{8,9},{9,8},{10,1... | collective-permute-start | bytes 393224 | tf_op jit(solution)/shard_map/ppermute | solution.py:353
  14.7 0.0 collective-permute-start.1
  14.7 0.5 %collective-permute-start.2 = (f32[16,16,128]{2,1,0:T(8,128)S(1)}, f32[16,16,128]{2,1,0:T(8,128)S(1)}, u32[]{:S(2)}, u32[]{:S(2)}) collective-permute-start(f32[16,16,128]{2,1,0:T(8,128)S(1)} %shard_map.48.own_ref.refs_0_), channel_id=1, source_target_pairs={{0,3},{1,0},{2,1},{3,2},{4,7},{5,4},{6,5},{7,6},{8,11},{9,8},{10,9... | collective-permute-start | bytes 393224 | tf_op jit(solution)/shard_map/ppermute | solution.py:329
  15.2 1.4 %collective-permute-done.3.first_ref = f32[16,16,128]{2,1,0:T(8,128)S(1)} collective-permute-done((f32[16,16,128]{2,1,0:T(8,128)S(1)}, f32[16,16,128]{2,1,0:T(8,128)S(1)}, u32[]{:S(2)}, u32[]{:S(2)}) %collective-permute-start.3) | collective-permute-done | bytes 131104 | tf_op jit(solution)/shard_map/ppermute | solution.py:353
  16.6 0.0 collective-permute-done.1.near_ref.refs_1_
  16.6 0.0 collective-permute-start.4
  16.7 2.6 %collective-permute-start.6 = (f32[16,16,128]{2,1,0:T(8,128)S(1)}, f32[16,16,128]{2,1,0:T(8,128)S(1)}, u32[]{:S(2)}, u32[]{:S(2)}) collective-permute-start(f32[16,16,128]{2,1,0:T(8,128)S(1)} %get-tuple-element.25), channel_id=1, source_target_pairs={{0,1},{1,2},{2,0},{3,7},{4,5},{5,4},{6,3},{7,6},{8,9},{9,8},{10,11... | collective-permute-start | bytes 393224 | tf_op jit(solution)/shard_map/ppermute | solution.py:377
  19.2 0.1 collective-permute-start.5
  19.3 0.0 collective-permute-done.2.refs_3_.far_ref
  19.3 1.2 %collective-permute-done.4.refs_4_.side_ref = f32[16,16,128]{2,1,0:T(8,128)S(1)} collective-permute-done((f32[16,16,128]{2,1,0:T(8,128)S(1)}, f32[16,16,128]{2,1,0:T(8,128)S(1)}, u32[]{:S(2)}, u32[]{:S(2)}) %collective-permute-start.4) | collective-permute-done | bytes 131104 | tf_op jit(solution)/shard_map/ppermute | solution.py:329
  20.5 0.0 collective-permute-done.6.refs_6_
  20.5 0.1 collective-permute-done.5.refs_5_
  20.6 3.6 %collective-permute-start.7 = (f32[16,16,128]{2,1,0:T(8,128)S(1)}, f32[16,16,128]{2,1,0:T(8,128)S(1)}, u32[]{:S(2)}, u32[]{:S(2)}) collective-permute-start(f32[16,16,128]{2,1,0:T(8,128)S(1)} %get-tuple-element.27), channel_id=1, source_target_pairs={{0,1},{1,0},{2,3},{3,2},{4,5},{5,9},{6,7},{7,11},{8,4},{9,8},{10,6... | collective-permute-start | bytes 393224 | tf_op jit(solution)/shard_map/ppermute | solution.py:349
  24.2 1.0 %collective-permute-done.7.refs_5_ = f32[16,16,128]{2,1,0:T(8,128)S(1)} collective-permute-done((f32[16,16,128]{2,1,0:T(8,128)S(1)}, f32[16,16,128]{2,1,0:T(8,128)S(1)}, u32[]{:S(2)}, u32[]{:S(2)}) %collective-permute-start.7) | collective-permute-done | bytes 131104 | tf_op jit(solution)/shard_map/ppermute | solution.py:349
  25.2 0.4 %collective-permute-start.8 = (f32[16,16,128]{2,1,0:T(8,128)S(1)}, f32[16,16,128]{2,1,0:T(8,128)S(1)}, u32[]{:S(2)}, u32[]{:S(2)}) collective-permute-start(f32[16,16,128]{2,1,0:T(8,128)S(1)} %get-tuple-element.29), channel_id=1, source_target_pairs={{0,1},{1,0},{2,3},{3,2},{4,5},{5,4},{6,7},{7,6},{8,9},{9,13},{10,1... | collective-permute-start | bytes 393224 | tf_op jit(solution)/shard_map/ppermute | solution.py:349
  25.5 5.8 %collective-permute-done.8.incoming_ref = f32[16,16,128]{2,1,0:T(8,128)S(1)} collective-permute-done((f32[16,16,128]{2,1,0:T(8,128)S(1)}, f32[16,16,128]{2,1,0:T(8,128)S(1)}, u32[]{:S(2)}, u32[]{:S(2)}) %collective-permute-start.8) | collective-permute-done | bytes 131104 | tf_op jit(solution)/shard_map/ppermute | solution.py:349
  31.4 0.1 collective-permute-start.9
  31.5 1.0 %shard_map.53 = (f32[5,16,16,128]{3,2,1,0:T(8,128)S(1)}, f32[16,16,128]{2,1,0:T(8,128)S(1)}) custom-call(f32[16,16,128]{2,1,0:T(8,128)S(1)} %shard_map.48.own_ref.refs_0_, f32[16,16,128]{2,1,0:T(8,128)S(1)} %collective-permute-done.1.near_ref.refs_1_, bf16[16,384,256]{2,1,0:T(8,128)(2,1)S(1)} %shard_map.47.coarse_ref.refs_2_, ...), custom_call_target="tpu_custom_call", output_to_operand_aliasing={{0}: (3, {})} | custom-call | flops 1000000000 | bytes 1000000 | tf_op jit(solution)/shard_map/pallas_call | solution.py:358
  32.5 0.1 collective-permute-start.10
  32.6 0.2 collective-permute-done.9.swapped_ref
  32.8 1.4 %shard_map.54.steps_ref = f32[1024,128]{1,0:T(8,128)S(1)} custom-call(f32[5,16,16,128]{3,2,1,0:T(8,128)S(1)} %get-tuple-element.32.held_ref, f32[16,16,128]{2,1,0:T(8,128)S(1)} %collective-permute-done.9.swapped_ref, f32[1024,128]{1,0:T(8,128)S(1)} %bitcast.17, bf16[16,384,256]{2,1,0:T(8,128)(2,1)S(1)} %get-tuple-element.21.fine_ref), custom_call_target="tpu_custom_call" | custom-call | flops 1000000000 | bytes 1000000 | tf_op jit(solution)/shard_map/pallas_call | solution.py:393
  34.3 0.0 collective-permute-done.10.swapped_ref
  34.3 0.9 %shard_map.55 = f32[1024,128]{1,0:T(8,128)} custom-call(f32[1024,128]{1,0:T(8,128)S(1)} %shard_map.54.steps_ref, f32[5,16,16,128]{3,2,1,0:T(8,128)S(1)} %get-tuple-element.32.held_ref, f32[16,16,128]{2,1,0:T(8,128)S(1)} %collective-permute-done.10.swapped_ref), custom_call_target="tpu_custom_call" | custom-call | flops 1000000 | bytes 1000000 | tf_op jit(solution)/shard_map/pallas_call | solution.py:394
  (4 shorter events, 0.0 us)
Async XLA Ops:
  4.6 3.9 %collective-permute-start = (f32[16,16,128]{2,1,0:T(8,128)S(1)}, f32[16,16,128]{2,1,0:T(8,128)S(1)}, u32[]{:S(2)}, u32[]{:S(2)}) collective-permute-start(f32[16,16,128]{2,1,0:T(8,128)S(1)} %get-tuple-element.20), channel_id=1, source_target_pairs={{0,1},{1,2},{2,3},{3,4},{4,5},{5,6},{6,7},{7,8},{8,9},{9,10},{10,1... | collective-permute-start | bytes 393224 | tf_op jit(solution)/shard_map/ppermute | solution.py:329
  6.5 2.0 %copy-start = (f32[2,4,16384]{2,1,0:T(4,128)S(1)}, f32[2,4,16384]{2,1,0:T(4,128)}, u32[]{:S(2)}) copy-start(f32[2,4,16384]{2,1,0:T(4,128)} %param.5) | copy-start | bytes 1572868
  6.5 2.0 %copy-start.1 = (f32[2,16384]{1,0:T(2,128)S(1)}, f32[2,16384]{1,0:T(2,128)}, u32[]{:S(2)}) copy-start(f32[2,16384]{1,0:T(2,128)} %param.4) | copy-start | bytes 393220
  10.7 5.9 %collective-permute-start.3 = (f32[16,16,128]{2,1,0:T(8,128)S(1)}, f32[16,16,128]{2,1,0:T(8,128)S(1)}, u32[]{:S(2)}, u32[]{:S(2)}) collective-permute-start(f32[16,16,128]{2,1,0:T(8,128)S(1)} %shard_map.48.own_ref.refs_0_), channel_id=1, source_target_pairs={{0,12},{1,3},{2,1},{3,2},{4,5},{5,4},{6,7},{7,6},{8,9},{9,8},{10,1... | collective-permute-start | bytes 393224 | tf_op jit(solution)/shard_map/ppermute | solution.py:353
  14.7 2.0 %collective-permute-start.1 = (f32[16,16,128]{2,1,0:T(8,128)S(1)}, f32[16,16,128]{2,1,0:T(8,128)S(1)}, u32[]{:S(2)}, u32[]{:S(2)}) collective-permute-start(f32[16,16,128]{2,1,0:T(8,128)S(1)} %shard_map.48.own_ref.refs_0_), channel_id=1, source_target_pairs={{0,1},{1,0},{2,3},{3,2},{4,5},{5,4},{6,7},{7,6},{8,9},{9,8},{10,11... | collective-permute-start | bytes 393224 | tf_op jit(solution)/shard_map/ppermute | solution.py:329
  14.7 4.6 %collective-permute-start.2 = (f32[16,16,128]{2,1,0:T(8,128)S(1)}, f32[16,16,128]{2,1,0:T(8,128)S(1)}, u32[]{:S(2)}, u32[]{:S(2)}) collective-permute-start(f32[16,16,128]{2,1,0:T(8,128)S(1)} %shard_map.48.own_ref.refs_0_), channel_id=1, source_target_pairs={{0,3},{1,0},{2,1},{3,2},{4,7},{5,4},{6,5},{7,6},{8,11},{9,8},{10,9... | collective-permute-start | bytes 393224 | tf_op jit(solution)/shard_map/ppermute | solution.py:329
  16.6 3.8 %collective-permute-start.4 = (f32[16,16,128]{2,1,0:T(8,128)S(1)}, f32[16,16,128]{2,1,0:T(8,128)S(1)}, u32[]{:S(2)}, u32[]{:S(2)}) collective-permute-start(f32[16,16,128]{2,1,0:T(8,128)S(1)} %shard_map.48.own_ref.refs_0_), channel_id=1, source_target_pairs={{0,2},{1,3},{2,0},{3,1},{4,6},{5,7},{6,4},{7,5},{8,10},{9,11},{10,... | collective-permute-start | bytes 393224 | tf_op jit(solution)/shard_map/ppermute | solution.py:329
  16.7 3.8 %collective-permute-start.6 = (f32[16,16,128]{2,1,0:T(8,128)S(1)}, f32[16,16,128]{2,1,0:T(8,128)S(1)}, u32[]{:S(2)}, u32[]{:S(2)}) collective-permute-start(f32[16,16,128]{2,1,0:T(8,128)S(1)} %get-tuple-element.25), channel_id=1, source_target_pairs={{0,1},{1,2},{2,0},{3,7},{4,5},{5,4},{6,3},{7,6},{8,9},{9,8},{10,11... | collective-permute-start | bytes 393224 | tf_op jit(solution)/shard_map/ppermute | solution.py:377
  19.2 1.3 %collective-permute-start.5 = (f32[16,16,128]{2,1,0:T(8,128)S(1)}, f32[16,16,128]{2,1,0:T(8,128)S(1)}, u32[]{:S(2)}, u32[]{:S(2)}) collective-permute-start(f32[16,16,128]{2,1,0:T(8,128)S(1)} %get-tuple-element.25), channel_id=1, source_target_pairs={{0,1},{1,2},{2,0},{3,5},{4,3},{5,4},{6,7},{7,6},{8,9},{9,8},{10,11... | collective-permute-start | bytes 393224 | tf_op jit(solution)/shard_map/ppermute | solution.py:377
  20.6 4.6 %collective-permute-start.7 = (f32[16,16,128]{2,1,0:T(8,128)S(1)}, f32[16,16,128]{2,1,0:T(8,128)S(1)}, u32[]{:S(2)}, u32[]{:S(2)}) collective-permute-start(f32[16,16,128]{2,1,0:T(8,128)S(1)} %get-tuple-element.27), channel_id=1, source_target_pairs={{0,1},{1,0},{2,3},{3,2},{4,5},{5,9},{6,7},{7,11},{8,4},{9,8},{10,6... | collective-permute-start | bytes 393224 | tf_op jit(solution)/shard_map/ppermute | solution.py:349
  25.2 6.2 %collective-permute-start.8 = (f32[16,16,128]{2,1,0:T(8,128)S(1)}, f32[16,16,128]{2,1,0:T(8,128)S(1)}, u32[]{:S(2)}, u32[]{:S(2)}) collective-permute-start(f32[16,16,128]{2,1,0:T(8,128)S(1)} %get-tuple-element.29), channel_id=1, source_target_pairs={{0,1},{1,0},{2,3},{3,2},{4,5},{5,4},{6,7},{7,6},{8,9},{9,13},{10,1... | collective-permute-start | bytes 393224 | tf_op jit(solution)/shard_map/ppermute | solution.py:349
  31.4 1.4 %collective-permute-start.9 = (f32[16,16,128]{2,1,0:T(8,128)S(1)}, f32[16,16,128]{2,1,0:T(8,128)S(1)}, u32[]{:S(2)}, u32[]{:S(2)}) collective-permute-start(f32[16,16,128]{2,1,0:T(8,128)S(1)} %get-tuple-element.33), channel_id=1, source_target_pairs={{0,1},{1,0},{2,3},{3,2},{4,5},{5,4},{6,7},{7,6},{8,9},{9,8},{10,11... | collective-permute-start | bytes 393224 | tf_op jit(solution)/shard_map/ppermute | solution.py:329
  32.5 1.8 %collective-permute-start.10 = (f32[16,16,128]{2,1,0:T(8,128)S(1)}, f32[16,16,128]{2,1,0:T(8,128)S(1)}, u32[]{:S(2)}, u32[]{:S(2)}) collective-permute-start(f32[16,16,128]{2,1,0:T(8,128)S(1)} %get-tuple-element.34), channel_id=1, source_target_pairs={{0,1},{1,0},{2,3},{3,2},{4,5},{5,4},{6,7},{7,6},{8,9},{9,8},{10,11... | collective-permute-start | bytes 393224 | tf_op jit(solution)/shard_map/ppermute | solution.py:329

commit v2 on v1

--- a/solution.py
+++ b/solution.py
@@ -371,13 +371,13 @@
     behind, following = lax.optimization_barrier((right, following))
     side = sent(behind, lambda i: i ^ 2, lambda i: i ^ 2)
 
-    def entered(chip):
+    def entered(**moves):
         target = {i: i ^ 1 for i in range(count)}
-        target.update({3: 2 * chip + 1, 2 * chip + 1: 2 * chip, 2 * chip: 3, 2: 0, 0: 1, 1: 2})
+        target.update({int(i[1:]): to for i, to in moves.items()})
         return lax.ppermute(following, "tm", list(target.items()))
 
-    across = entered(2)
-    along = entered(3)
+    across = entered(d3=5, d5=4, d4=2, d2=3, d7=11, d11=7, d6=10, d10=6)
+    along = entered(d3=7, d7=6, d6=3, d2=0, d0=1, d1=2)
     incoming = (across, along)
     last = count // 4 - 1
     for turn in range(1, last):

time: 35.3 us -> 36.4 us (1.031)
  the two profiles are of different devices: /device:TPU:71 before, /device:TPU:53 now
where the time goes in v2:
time: 36.4 us; the launch traced here: 36.3 us
  waiting for transfers between devices  14.9 us (41%)
  Pallas kernels  11.9 us (33%)
  starting transfers between devices  9.45 us (26%)
    ppermute x2, waiting for transfers between devices, relayed(): return lax.ppermute(value, 'tm', list(target.items()))  7.49 us
    ppermute x6, waiting for transfers between devices, sent(): lax.ppermute(value, 'tm', [(i, (odd if i % 2 else even)(i) % count) for i...  6.9 us
    ppermute x6, starting transfers between devices, sent(): lax.ppermute(value, 'tm', [(i, (odd if i % 2 else even)(i) % count) for i...  4.87 us
    pallas_call x1, Pallas kernels, body(): call(relax_kernel, [HBM] * 4, [full, weights, jax.ShapeDtypeStruct(coarse...  4.61 us
    ppermute x1, starting transfers between devices, body(): first = lax.ppermute(right, 'tm', list(urgent.items()))  2.53 us
    pallas_call x1, Pallas kernels, body(): call(residual_kernel, [VMEM] * 5, full, states(zones, rows) + [pltpu.VMEM...  2.23 us
    pallas_call x5, Pallas kernels, chain(): call(kernel, [VMEM] * (len(inputs) + (held is not None)), [held_states] +...  1.82 us
    pallas_call x1, Pallas kernels, body(): call(final_kernel, [VMEM] * 4, forces, states(zones, rows), 10, 10 ** 9)  1.43 us
  transfers between devices with their start and end apart: 11, of which 8 were waited for; matrix products, arithmetic and copies ran while one was open for 0% of the time, Pallas kernels for 6%

profile of v2, /device:TPU:53, one launch (start us, length us, event | category | flops | bytes accessed | tf_op | source)
XLA Modules:
  0.0 36.3 jit_solution(15288780456209955759)
XLA Ops:
  0.0 4.6 %shard_map.46 = (f32[16,16,128]{2,1,0:T(8,128)S(1)}, bf16[16,384,256]{2,1,0:T(8,128)(2,1)S(1)}, f32[16,3,128,128]{3,2,1,0:T(8,128)S(1)}) custom-call(f32[256,128]{1,0:T(8,128)} %bitcast.18, f32[1024,128]{1,0:T(8,128)} %bitcast.15, f32[16,3,128,128]{3,2,1,0:T(8,128)} %blocks_ref.1, f32[16,3,128,128]{3,2,1,0:T(8,128)} %next_blocks_ref.1), custom_call_target="tpu_custom_call" | custom-call | flops 1000000000 | bytes 1000000 | tf_op jit(solution)/shard_map/pallas_call | solution.py:333
  4.6 1.6 %collective-permute-start = (f32[16,16,128]{2,1,0:T(8,128)S(1)}, f32[16,16,128]{2,1,0:T(8,128)S(1)}, u32[]{:S(2)}, u32[]{:S(2)}) collective-permute-start(f32[16,16,128]{2,1,0:T(8,128)S(1)} %get-tuple-element.20), channel_id=1, source_target_pairs={{0,1},{1,2},{2,3},{3,4},{4,5},{5,6},{6,7},{7,8},{8,9},{9,10},{10,1... | collective-permute-start | bytes 393224 | tf_op jit(solution)/shard_map/ppermute | solution.py:329
  6.3 0.0 copy-start
  6.3 0.0 copy-start.1
  6.3 0.9 %shard_map.47.coarse_ref.refs_2_ = bf16[16,384,256]{2,1,0:T(8,128)(2,1)S(1)} custom-call(f32[16,3,128,128]{3,2,1,0:T(8,128)S(1)} %get-tuple-element.22.blocks_ref), custom_call_target="tpu_custom_call" | custom-call | flops 1000000000 | bytes 1000000 | tf_op jit(solution)/shard_map/pallas_call | solution.py:339
  7.1 1.1 %collective-permute-done.carried_ref.before_ref = f32[16,16,128]{2,1,0:T(8,128)S(1)} collective-permute-done((f32[16,16,128]{2,1,0:T(8,128)S(1)}, f32[16,16,128]{2,1,0:T(8,128)S(1)}, u32[]{:S(2)}, u32[]{:S(2)}) %collective-permute-start) | collective-permute-done | bytes 131104 | tf_op jit(solution)/shard_map/ppermute | solution.py:329
  8.2 0.0 copy-done
  8.2 0.0 copy-done.1
  8.2 2.2 %shard_map.48.own_ref.refs_0_ = f32[16,16,128]{2,1,0:T(8,128)S(1)} custom-call(f32[256,128]{1,0:T(8,128)S(1)} %bitcast.19, f32[16,16,128]{2,1,0:T(8,128)S(1)} %collective-permute-done.carried_ref.before_ref, f32[1024,128]{1,0:T(8,128)S(1)} %bitcast.16, bf16[16,384,256]{2,1,0:T(8,128)(2,1)S(1)} %get-tuple-element.21.fine_ref, ...), custom_call_target="tpu_custom_call" | custom-call | flops 1000000000 | bytes 1000000 | tf_op jit(solution)/shard_map/pallas_call | solution.py:340
  10.4 2.5 %collective-permute-start.3 = (f32[16,16,128]{2,1,0:T(8,128)S(1)}, f32[16,16,128]{2,1,0:T(8,128)S(1)}, u32[]{:S(2)}, u32[]{:S(2)}) collective-permute-start(f32[16,16,128]{2,1,0:T(8,128)S(1)} %shard_map.48.own_ref.refs_0_), channel_id=1, source_target_pairs={{0,12},{1,3},{2,1},{3,2},{4,5},{5,4},{6,7},{7,6},{8,9},{9,8},{10,1... | collective-permute-start | bytes 393224 | tf_op jit(solution)/shard_map/ppermute | solution.py:353
  13.0 0.1 collective-permute-start.1
  13.1 0.4 %collective-permute-start.2 = (f32[16,16,128]{2,1,0:T(8,128)S(1)}, f32[16,16,128]{2,1,0:T(8,128)S(1)}, u32[]{:S(2)}, u32[]{:S(2)}) collective-permute-start(f32[16,16,128]{2,1,0:T(8,128)S(1)} %shard_map.48.own_ref.refs_0_), channel_id=1, source_target_pairs={{0,3},{1,0},{2,1},{3,2},{4,7},{5,4},{6,5},{7,6},{8,11},{9,8},{10,9... | collective-permute-start | bytes 393224 | tf_op jit(solution)/shard_map/ppermute | solution.py:329
  13.5 0.5 %collective-permute-done.3.first_ref = f32[16,16,128]{2,1,0:T(8,128)S(1)} collective-permute-done((f32[16,16,128]{2,1,0:T(8,128)S(1)}, f32[16,16,128]{2,1,0:T(8,128)S(1)}, u32[]{:S(2)}, u32[]{:S(2)}) %collective-permute-start.3) | collective-permute-done | bytes 131104 | tf_op jit(solution)/shard_map/ppermute | solution.py:353
  14.0 0.4 collective-permute-done.1.near_ref.refs_1_
  14.3 0.1 collective-permute-start.4
  14.4 0.8 %collective-permute-start.6 = (f32[16,16,128]{2,1,0:T(8,128)S(1)}, f32[16,16,128]{2,1,0:T(8,128)S(1)}, u32[]{:S(2)}, u32[]{:S(2)}) collective-permute-start(f32[16,16,128]{2,1,0:T(8,128)S(1)} %get-tuple-element.25), channel_id=1, source_target_pairs={{0,1},{1,2},{2,0},{3,7},{4,5},{5,4},{6,3},{7,6},{8,9},{9,8},{10,11... | collective-permute-start | bytes 393224 | tf_op jit(solution)/shard_map/ppermute | solution.py:377
  15.2 0.0 collective-permute-start.5
  15.2 3.0 %collective-permute-done.2.refs_3_.far_ref = f32[16,16,128]{2,1,0:T(8,128)S(1)} collective-permute-done((f32[16,16,128]{2,1,0:T(8,128)S(1)}, f32[16,16,128]{2,1,0:T(8,128)S(1)}, u32[]{:S(2)}, u32[]{:S(2)}) %collective-permute-start.2) | collective-permute-done | bytes 131104 | tf_op jit(solution)/shard_map/ppermute | solution.py:329
  18.2 1.7 %collective-permute-done.4.refs_4_.side_ref = f32[16,16,128]{2,1,0:T(8,128)S(1)} collective-permute-done((f32[16,16,128]{2,1,0:T(8,128)S(1)}, f32[16,16,128]{2,1,0:T(8,128)S(1)}, u32[]{:S(2)}, u32[]{:S(2)}) %collective-permute-start.4) | collective-permute-done | bytes 131104 | tf_op jit(solution)/shard_map/ppermute | solution.py:329
  19.8 0.0 collective-permute-done.6.refs_6_
  19.8 0.0 collective-permute-done.5.refs_5_
  19.8 1.2 %collective-permute-start.7 = (f32[16,16,128]{2,1,0:T(8,128)S(1)}, f32[16,16,128]{2,1,0:T(8,128)S(1)}, u32[]{:S(2)}, u32[]{:S(2)}) collective-permute-start(f32[16,16,128]{2,1,0:T(8,128)S(1)} %get-tuple-element.27), channel_id=1, source_target_pairs={{0,1},{1,0},{2,3},{3,2},{4,5},{5,9},{6,7},{7,11},{8,4},{9,8},{10,6... | collective-permute-start | bytes 393224 | tf_op jit(solution)/shard_map/ppermute | solution.py:349
  21.0 5.5 %collective-permute-done.7.refs_5_ = f32[16,16,128]{2,1,0:T(8,128)S(1)} collective-permute-done((f32[16,16,128]{2,1,0:T(8,128)S(1)}, f32[16,16,128]{2,1,0:T(8,128)S(1)}, u32[]{:S(2)}, u32[]{:S(2)}) %collective-permute-start.7) | collective-permute-done | bytes 131104 | tf_op jit(solution)/shard_map/ppermute | solution.py:349
  26.6 1.8 %shard_map.51 = (f32[5,16,16,128]{3,2,1,0:T(8,128)S(1)}, f32[16,16,128]{2,1,0:T(8,128)S(1)}) custom-call(f32[16,16,128]{2,1,0:T(8,128)S(1)} %shard_map.48.own_ref.refs_0_, f32[16,16,128]{2,1,0:T(8,128)S(1)} %collective-permute-done.1.near_ref.refs_1_, bf16[16,384,256]{2,1,0:T(8,128)(2,1)S(1)} %shard_map.47.coarse_ref.refs_2_, ...), custom_call_target="tpu_custom_call", output_to_operand_aliasing={{0}: (6, {})} | custom-call | flops 1000000000 | bytes 1000000 | tf_op jit(solution)/shard_map/pallas_call | solution.py:358
  28.4 0.1 collective-permute-start.8
  28.5 1.9 %collective-permute-done.8.incoming_ref = f32[16,16,128]{2,1,0:T(8,128)S(1)} collective-permute-done((f32[16,16,128]{2,1,0:T(8,128)S(1)}, f32[16,16,128]{2,1,0:T(8,128)S(1)}, u32[]{:S(2)}, u32[]{:S(2)}) %collective-permute-start.8) | collective-permute-done | bytes 131104 | tf_op jit(solution)/shard_map/ppermute | solution.py:349
  30.4 2.5 %collective-permute-start.9 = (f32[16,16,128]{2,1,0:T(8,128)S(1)}, f32[16,16,128]{2,1,0:T(8,128)S(1)}, u32[]{:S(2)}, u32[]{:S(2)}) collective-permute-start(f32[16,16,128]{2,1,0:T(8,128)S(1)} %get-tuple-element.33), channel_id=1, source_target_pairs={{0,1},{1,0},{2,3},{3,2},{4,5},{5,4},{6,7},{7,6},{8,9},{9,8},{10,11... | collective-permute-start | bytes 393224 | tf_op jit(solution)/shard_map/ppermute | solution.py:329
  32.9 0.1 collective-permute-start.10
  33.1 0.9 %collective-permute-done.9.swapped_ref = f32[16,16,128]{2,1,0:T(8,128)S(1)} collective-permute-done((f32[16,16,128]{2,1,0:T(8,128)S(1)}, f32[16,16,128]{2,1,0:T(8,128)S(1)}, u32[]{:S(2)}, u32[]{:S(2)}) %collective-permute-start.9) | collective-permute-done | bytes 131104 | tf_op jit(solution)/shard_map/ppermute | solution.py:329
  33.9 1.4 %shard_map.54.steps_ref = f32[1024,128]{1,0:T(8,128)S(1)} custom-call(f32[5,16,16,128]{3,2,1,0:T(8,128)S(1)} %get-tuple-element.32.held_ref, f32[16,16,128]{2,1,0:T(8,128)S(1)} %collective-permute-done.9.swapped_ref, f32[1024,128]{1,0:T(8,128)S(1)} %bitcast.17, bf16[16,384,256]{2,1,0:T(8,128)(2,1)S(1)} %get-tuple-element.21.fine_ref), custom_call_target="tpu_custom_call" | custom-call | flops 1000000000 | bytes 1000000 | tf_op jit(solution)/shard_map/pallas_call | solution.py:393
  35.4 0.0 collective-permute-done.10.swapped_ref
  35.4 0.9 %shard_map.55 = f32[1024,128]{1,0:T(8,128)} custom-call(f32[1024,128]{1,0:T(8,128)S(1)} %shard_map.54.steps_ref, f32[5,16,16,128]{3,2,1,0:T(8,128)S(1)} %get-tuple-element.32.held_ref, f32[16,16,128]{2,1,0:T(8,128)S(1)} %collective-permute-done.10.swapped_ref), custom_call_target="tpu_custom_call" | custom-call | flops 1000000 | bytes 1000000 | tf_op jit(solution)/shard_map/pallas_call | solution.py:394
  (4 shorter events, 0.0 us)
Async XLA Ops:
  4.6 3.6 %collective-permute-start = (f32[16,16,128]{2,1,0:T(8,128)S(1)}, f32[16,16,128]{2,1,0:T(8,128)S(1)}, u32[]{:S(2)}, u32[]{:S(2)}) collective-permute-start(f32[16,16,128]{2,1,0:T(8,128)S(1)} %get-tuple-element.20), channel_id=1, source_target_pairs={{0,1},{1,2},{2,3},{3,4},{4,5},{5,6},{6,7},{7,8},{8,9},{9,10},{10,1... | collective-permute-start | bytes 393224 | tf_op jit(solution)/shard_map/ppermute | solution.py:329
  6.3 2.0 %copy-start = (f32[2,4,16384]{2,1,0:T(4,128)S(1)}, f32[2,4,16384]{2,1,0:T(4,128)}, u32[]{:S(2)}) copy-start(f32[2,4,16384]{2,1,0:T(4,128)} %param.5) | copy-start | bytes 1572868
  6.3 2.0 %copy-start.1 = (f32[2,16384]{1,0:T(2,128)S(1)}, f32[2,16384]{1,0:T(2,128)}, u32[]{:S(2)}) copy-start(f32[2,16384]{1,0:T(2,128)} %param.4) | copy-start | bytes 393220
  10.4 3.5 %collective-permute-start.3 = (f32[16,16,128]{2,1,0:T(8,128)S(1)}, f32[16,16,128]{2,1,0:T(8,128)S(1)}, u32[]{:S(2)}, u32[]{:S(2)}) collective-permute-start(f32[16,16,128]{2,1,0:T(8,128)S(1)} %shard_map.48.own_ref.refs_0_), channel_id=1, source_target_pairs={{0,12},{1,3},{2,1},{3,2},{4,5},{5,4},{6,7},{7,6},{8,9},{9,8},{10,1... | collective-permute-start | bytes 393224 | tf_op jit(solution)/shard_map/ppermute | solution.py:353
  13.0 1.3 %collective-permute-start.1 = (f32[16,16,128]{2,1,0:T(8,128)S(1)}, f32[16,16,128]{2,1,0:T(8,128)S(1)}, u32[]{:S(2)}, u32[]{:S(2)}) collective-permute-start(f32[16,16,128]{2,1,0:T(8,128)S(1)} %shard_map.48.own_ref.refs_0_), channel_id=1, source_target_pairs={{0,1},{1,0},{2,3},{3,2},{4,5},{5,4},{6,7},{7,6},{8,9},{9,8},{10,11... | collective-permute-start | bytes 393224 | tf_op jit(solution)/shard_map/ppermute | solution.py:329
  13.1 5.1 %collective-permute-start.2 = (f32[16,16,128]{2,1,0:T(8,128)S(1)}, f32[16,16,128]{2,1,0:T(8,128)S(1)}, u32[]{:S(2)}, u32[]{:S(2)}) collective-permute-start(f32[16,16,128]{2,1,0:T(8,128)S(1)} %shard_map.48.own_ref.refs_0_), channel_id=1, source_target_pairs={{0,3},{1,0},{2,1},{3,2},{4,7},{5,4},{6,5},{7,6},{8,11},{9,8},{10,9... | collective-permute-start | bytes 393224 | tf_op jit(solution)/shard_map/ppermute | solution.py:329
  14.3 5.5 %collective-permute-start.4 = (f32[16,16,128]{2,1,0:T(8,128)S(1)}, f32[16,16,128]{2,1,0:T(8,128)S(1)}, u32[]{:S(2)}, u32[]{:S(2)}) collective-permute-start(f32[16,16,128]{2,1,0:T(8,128)S(1)} %shard_map.48.own_ref.refs_0_), channel_id=1, source_target_pairs={{0,2},{1,3},{2,0},{3,1},{4,6},{5,7},{6,4},{7,5},{8,10},{9,11},{10,... | collective-permute-start | bytes 393224 | tf_op jit(solution)/shard_map/ppermute | solution.py:329
  14.4 5.4 %collective-permute-start.6 = (f32[16,16,128]{2,1,0:T(8,128)S(1)}, f32[16,16,128]{2,1,0:T(8,128)S(1)}, u32[]{:S(2)}, u32[]{:S(2)}) collective-permute-start(f32[16,16,128]{2,1,0:T(8,128)S(1)} %get-tuple-element.25), channel_id=1, source_target_pairs={{0,1},{1,2},{2,0},{3,7},{4,5},{5,4},{6,3},{7,6},{8,9},{9,8},{10,11... | collective-permute-start | bytes 393224 | tf_op jit(solution)/shard_map/ppermute | solution.py:377
  15.2 4.6 %collective-permute-start.5 = (f32[16,16,128]{2,1,0:T(8,128)S(1)}, f32[16,16,128]{2,1,0:T(8,128)S(1)}, u32[]{:S(2)}, u32[]{:S(2)}) collective-permute-start(f32[16,16,128]{2,1,0:T(8,128)S(1)} %get-tuple-element.25), channel_id=1, source_target_pairs={{0,1},{1,0},{2,3},{3,5},{4,2},{5,4},{6,10},{7,11},{8,9},{9,8},{10,... | collective-permute-start | bytes 393224 | tf_op jit(solution)/shard_map/ppermute | solution.py:377
  19.8 6.7 %collective-permute-start.7 = (f32[16,16,128]{2,1,0:T(8,128)S(1)}, f32[16,16,128]{2,1,0:T(8,128)S(1)}, u32[]{:S(2)}, u32[]{:S(2)}) collective-permute-start(f32[16,16,128]{2,1,0:T(8,128)S(1)} %get-tuple-element.27), channel_id=1, source_target_pairs={{0,1},{1,0},{2,3},{3,2},{4,5},{5,9},{6,7},{7,11},{8,4},{9,8},{10,6... | collective-permute-start | bytes 393224 | tf_op jit(solution)/shard_map/ppermute | solution.py:349
  28.4 2.0 %collective-permute-start.8 = (f32[16,16,128]{2,1,0:T(8,128)S(1)}, f32[16,16,128]{2,1,0:T(8,128)S(1)}, u32[]{:S(2)}, u32[]{:S(2)}) collective-permute-start(f32[16,16,128]{2,1,0:T(8,128)S(1)} %get-tuple-element.29), channel_id=1, source_target_pairs={{0,1},{1,0},{2,3},{3,2},{4,5},{5,4},{6,7},{7,6},{8,9},{9,13},{10,1... | collective-permute-start | bytes 393224 | tf_op jit(solution)/shard_map/ppermute | solution.py:349
  30.4 3.5 %collective-permute-start.9 = (f32[16,16,128]{2,1,0:T(8,128)S(1)}, f32[16,16,128]{2,1,0:T(8,128)S(1)}, u32[]{:S(2)}, u32[]{:S(2)}) collective-permute-start(f32[16,16,128]{2,1,0:T(8,128)S(1)} %get-tuple-element.33), channel_id=1, source_target_pairs={{0,1},{1,0},{2,3},{3,2},{4,5},{5,4},{6,7},{7,6},{8,9},{9,8},{10,11... | collective-permute-start | bytes 393224 | tf_op jit(solution)/shard_map/ppermute | solution.py:329
  32.9 2.4 %collective-permute-start.10 = (f32[16,16,128]{2,1,0:T(8,128)S(1)}, f32[16,16,128]{2,1,0:T(8,128)S(1)}, u32[]{:S(2)}, u32[]{:S(2)}) collective-permute-start(f32[16,16,128]{2,1,0:T(8,128)S(1)} %get-tuple-element.34), channel_id=1, source_target_pairs={{0,1},{1,0},{2,3},{3,2},{4,5},{5,4},{6,7},{7,6},{8,9},{9,8},{10,11... | collective-permute-start | bytes 393224 | tf_op jit(solution)/shard_map/ppermute | solution.py:329

commit v3 on v2

--- a/solution.py
+++ b/solution.py
@@ -342,10 +342,10 @@
         states(zones, rows) + [pltpu.VMEM((zones, rows, BLK), F32)], 14, 10**9,
     )(start, carried, force, fine, coarse)
 
-    def relayed(value, moves):
+    def relayed(value, turn):
         target = {i: i ^ 1 for i in range(count)}
-        for a, b in moves:
-            target.update({2 * a + 1: 2 * b + 1, 2 * b + 1: 2 * b, 2 * b: 2 * a, 2 * a: 2 * a + 1})
+        for i in (4 * turn, 4 * turn + 2):
+            target.update({i + 1: i + 5, i + 5: i + 4, i + 4: i + 1, i: i ^ 2})
         return lax.ppermute(value, "tm", list(target.items()))
 
     urgent = {i: i ^ 1 for i in range(count)}
@@ -383,7 +383,7 @@
     for turn in range(1, last):
         held, following = chain(
             middle(turn, len(incoming)), (right, near, coarse, far, side, *incoming), 1, held)
-        incoming = (relayed(following, [(2 * turn + y, 2 * turn + 2 + y) for y in range(2)]),)
+        incoming = (relayed(following, turn),)
     held, give = chain(
         functools.partial(enter_kernel, last), (*incoming, far, side, coarse), 1, held)
     swapped = sent(give, lambda i: i ^ 1, lambda i: i ^ 1)

time: 36.4 us -> 36.8 us (1.011)
  the two profiles are of different devices: /device:TPU:53 before, /device:TPU:21 now
where the time goes in v3:
time: 36.8 us; the launch traced here: 36.7 us
  waiting for transfers between devices  17.2 us (47%)
  Pallas kernels  11.9 us (32%)
  starting transfers between devices  7.46 us (20%)
    ppermute x2, waiting for transfers between devices, relayed(): return lax.ppermute(value, 'tm', list(target.items()))  9.93 us
    ppermute x6, waiting for transfers between devices, sent(): lax.ppermute(value, 'tm', [(i, (odd if i % 2 else even)(i) % count) for i...  6.79 us
    pallas_call x1, Pallas kernels, body(): call(relax_kernel, [HBM] * 4, [full, weights, jax.ShapeDtypeStruct(coarse...  4.61 us
    ppermute x6, starting transfers between devices, sent(): lax.ppermute(value, 'tm', [(i, (odd if i % 2 else even)(i) % count) for i...  2.89 us
    ppermute x1, starting transfers between devices, body(): first = lax.ppermute(right, 'tm', list(urgent.items()))  2.53 us
    pallas_call x1, Pallas kernels, body(): call(residual_kernel, [VMEM] * 5, full, states(zones, rows) + [pltpu.VMEM...  2.23 us
    pallas_call x5, Pallas kernels, chain(): call(kernel, [VMEM] * (len(inputs) + (held is not None)), [held_states] +...  1.84 us
    pallas_call x1, Pallas kernels, body(): call(final_kernel, [VMEM] * 4, forces, states(zones, rows), 10, 10 ** 9)  1.43 us
  transfers between devices with their start and end apart: 11, of which 8 were waited for; matrix products, arithmetic and copies ran while one was open for 0% of the time, Pallas kernels for 6%

profile of v3, /device:TPU:21, one launch (start us, length us, event | category | flops | bytes accessed | tf_op | source)
XLA Modules:
  0.0 36.7 jit_solution(9490437645291847496)
XLA Ops:
  0.0 4.6 %shard_map.46 = (f32[16,16,128]{2,1,0:T(8,128)S(1)}, bf16[16,384,256]{2,1,0:T(8,128)(2,1)S(1)}, f32[16,3,128,128]{3,2,1,0:T(8,128)S(1)}) custom-call(f32[256,128]{1,0:T(8,128)} %bitcast.18, f32[1024,128]{1,0:T(8,128)} %bitcast.15, f32[16,3,128,128]{3,2,1,0:T(8,128)} %blocks_ref.1, f32[16,3,128,128]{3,2,1,0:T(8,128)} %next_blocks_ref.1), custom_call_target="tpu_custom_call" | custom-call | flops 1000000000 | bytes 1000000 | tf_op jit(solution)/shard_map/pallas_call | solution.py:333
  4.6 1.6 %collective-permute-start = (f32[16,16,128]{2,1,0:T(8,128)S(1)}, f32[16,16,128]{2,1,0:T(8,128)S(1)}, u32[]{:S(2)}, u32[]{:S(2)}) collective-permute-start(f32[16,16,128]{2,1,0:T(8,128)S(1)} %get-tuple-element.20), channel_id=1, source_target_pairs={{0,1},{1,2},{2,3},{3,4},{4,5},{5,6},{6,7},{7,8},{8,9},{9,10},{10,1... | collective-permute-start | bytes 393224 | tf_op jit(solution)/shard_map/ppermute | solution.py:329
  6.3 0.0 copy-start
  6.3 0.0 copy-start.1
  6.3 0.9 %shard_map.47.coarse_ref.refs_2_ = bf16[16,384,256]{2,1,0:T(8,128)(2,1)S(1)} custom-call(f32[16,3,128,128]{3,2,1,0:T(8,128)S(1)} %get-tuple-element.22.blocks_ref), custom_call_target="tpu_custom_call" | custom-call | flops 1000000000 | bytes 1000000 | tf_op jit(solution)/shard_map/pallas_call | solution.py:339
  7.1 1.1 %collective-permute-done.carried_ref.before_ref = f32[16,16,128]{2,1,0:T(8,128)S(1)} collective-permute-done((f32[16,16,128]{2,1,0:T(8,128)S(1)}, f32[16,16,128]{2,1,0:T(8,128)S(1)}, u32[]{:S(2)}, u32[]{:S(2)}) %collective-permute-start) | collective-permute-done | bytes 131104 | tf_op jit(solution)/shard_map/ppermute | solution.py:329
  8.2 0.0 copy-done
  8.2 0.0 copy-done.1
  8.2 2.2 %shard_map.48.own_ref.refs_0_ = f32[16,16,128]{2,1,0:T(8,128)S(1)} custom-call(f32[256,128]{1,0:T(8,128)S(1)} %bitcast.19, f32[16,16,128]{2,1,0:T(8,128)S(1)} %collective-permute-done.carried_ref.before_ref, f32[1024,128]{1,0:T(8,128)S(1)} %bitcast.16, bf16[16,384,256]{2,1,0:T(8,128)(2,1)S(1)} %get-tuple-element.21.fine_ref, ...), custom_call_target="tpu_custom_call" | custom-call | flops 1000000000 | bytes 1000000 | tf_op jit(solution)/shard_map/pallas_call | solution.py:340
  10.4 2.5 %collective-permute-start.3 = (f32[16,16,128]{2,1,0:T(8,128)S(1)}, f32[16,16,128]{2,1,0:T(8,128)S(1)}, u32[]{:S(2)}, u32[]{:S(2)}) collective-permute-start(f32[16,16,128]{2,1,0:T(8,128)S(1)} %shard_map.48.own_ref.refs_0_), channel_id=1, source_target_pairs={{0,12},{1,3},{2,1},{3,2},{4,5},{5,4},{6,7},{7,6},{8,9},{9,8},{10,1... | collective-permute-start | bytes 393224 | tf_op jit(solution)/shard_map/ppermute | solution.py:353
  13.0 0.1 collective-permute-start.1
  13.1 0.4 %collective-permute-start.2 = (f32[16,16,128]{2,1,0:T(8,128)S(1)}, f32[16,16,128]{2,1,0:T(8,128)S(1)}, u32[]{:S(2)}, u32[]{:S(2)}) collective-permute-start(f32[16,16,128]{2,1,0:T(8,128)S(1)} %shard_map.48.own_ref.refs_0_), channel_id=1, source_target_pairs={{0,3},{1,0},{2,1},{3,2},{4,7},{5,4},{6,5},{7,6},{8,11},{9,8},{10,9... | collective-permute-start | bytes 393224 | tf_op jit(solution)/shard_map/ppermute | solution.py:329
  13.5 0.5 %collective-permute-done.3.first_ref = f32[16,16,128]{2,1,0:T(8,128)S(1)} collective-permute-done((f32[16,16,128]{2,1,0:T(8,128)S(1)}, f32[16,16,128]{2,1,0:T(8,128)S(1)}, u32[]{:S(2)}, u32[]{:S(2)}) %collective-permute-start.3) | collective-permute-done | bytes 131104 | tf_op jit(solution)/shard_map/ppermute | solution.py:353
  14.0 0.4 collective-permute-done.1.near_ref.refs_1_
  14.3 0.1 collective-permute-start.4
  14.4 0.8 %collective-permute-start.6 = (f32[16,16,128]{2,1,0:T(8,128)S(1)}, f32[16,16,128]{2,1,0:T(8,128)S(1)}, u32[]{:S(2)}, u32[]{:S(2)}) collective-permute-start(f32[16,16,128]{2,1,0:T(8,128)S(1)} %get-tuple-element.25), channel_id=1, source_target_pairs={{0,1},{1,2},{2,0},{3,7},{4,5},{5,4},{6,3},{7,6},{8,9},{9,8},{10,11... | collective-permute-start | bytes 393224 | tf_op jit(solution)/shard_map/ppermute | solution.py:377
  15.2 0.0 collective-permute-start.5
  15.2 3.0 %collective-permute-done.2.refs_3_.far_ref = f32[16,16,128]{2,1,0:T(8,128)S(1)} collective-permute-done((f32[16,16,128]{2,1,0:T(8,128)S(1)}, f32[16,16,128]{2,1,0:T(8,128)S(1)}, u32[]{:S(2)}, u32[]{:S(2)}) %collective-permute-start.2) | collective-permute-done | bytes 131104 | tf_op jit(solution)/shard_map/ppermute | solution.py:329
  18.2 1.7 %collective-permute-done.4.refs_4_.side_ref = f32[16,16,128]{2,1,0:T(8,128)S(1)} collective-permute-done((f32[16,16,128]{2,1,0:T(8,128)S(1)}, f32[16,16,128]{2,1,0:T(8,128)S(1)}, u32[]{:S(2)}, u32[]{:S(2)}) %collective-permute-start.4) | collective-permute-done | bytes 131104 | tf_op jit(solution)/shard_map/ppermute | solution.py:329
  19.8 0.0 collective-permute-done.6.refs_6_
  19.8 0.0 collective-permute-done.5.refs_5_
  19.8 1.2 %collective-permute-start.7 = (f32[16,16,128]{2,1,0:T(8,128)S(1)}, f32[16,16,128]{2,1,0:T(8,128)S(1)}, u32[]{:S(2)}, u32[]{:S(2)}) collective-permute-start(f32[16,16,128]{2,1,0:T(8,128)S(1)} %get-tuple-element.27), channel_id=1, source_target_pairs={{0,1},{1,0},{2,3},{3,2},{4,6},{5,9},{6,4},{7,11},{8,5},{9,8},{10,7... | collective-permute-start | bytes 393224 | tf_op jit(solution)/shard_map/ppermute | solution.py:349
  21.0 5.5 %collective-permute-done.7.refs_5_ = f32[16,16,128]{2,1,0:T(8,128)S(1)} collective-permute-done((f32[16,16,128]{2,1,0:T(8,128)S(1)}, f32[16,16,128]{2,1,0:T(8,128)S(1)}, u32[]{:S(2)}, u32[]{:S(2)}) %collective-permute-start.7) | collective-permute-done | bytes 131104 | tf_op jit(solution)/shard_map/ppermute | solution.py:349
  26.6 1.8 %shard_map.51 = (f32[5,16,16,128]{3,2,1,0:T(8,128)S(1)}, f32[16,16,128]{2,1,0:T(8,128)S(1)}) custom-call(f32[16,16,128]{2,1,0:T(8,128)S(1)} %shard_map.48.own_ref.refs_0_, f32[16,16,128]{2,1,0:T(8,128)S(1)} %collective-permute-done.1.near_ref.refs_1_, bf16[16,384,256]{2,1,0:T(8,128)(2,1)S(1)} %shard_map.47.coarse_ref.refs_2_, ...), custom_call_target="tpu_custom_call", output_to_operand_aliasing={{0}: (6, {})} | custom-call | flops 1000000000 | bytes 1000000 | tf_op jit(solution)/shard_map/pallas_call | solution.py:358
  28.4 0.1 collective-permute-start.8
  28.5 4.4 %collective-permute-done.8.incoming_ref = f32[16,16,128]{2,1,0:T(8,128)S(1)} collective-permute-done((f32[16,16,128]{2,1,0:T(8,128)S(1)}, f32[16,16,128]{2,1,0:T(8,128)S(1)}, u32[]{:S(2)}, u32[]{:S(2)}) %collective-permute-start.8) | collective-permute-done | bytes 131104 | tf_op jit(solution)/shard_map/ppermute | solution.py:349
  32.9 0.1 collective-permute-start.9
  33.0 0.6 %collective-permute-start.10 = (f32[16,16,128]{2,1,0:T(8,128)S(1)}, f32[16,16,128]{2,1,0:T(8,128)S(1)}, u32[]{:S(2)}, u32[]{:S(2)}) collective-permute-start(f32[16,16,128]{2,1,0:T(8,128)S(1)} %get-tuple-element.34), channel_id=1, source_target_pairs={{0,1},{1,0},{2,3},{3,2},{4,5},{5,4},{6,7},{7,6},{8,9},{9,8},{10,11... | collective-permute-start | bytes 393224 | tf_op jit(solution)/shard_map/ppermute | solution.py:329
  33.5 0.7 %collective-permute-done.9.swapped_ref = f32[16,16,128]{2,1,0:T(8,128)S(1)} collective-permute-done((f32[16,16,128]{2,1,0:T(8,128)S(1)}, f32[16,16,128]{2,1,0:T(8,128)S(1)}, u32[]{:S(2)}, u32[]{:S(2)}) %collective-permute-start.9) | collective-permute-done | bytes 131104 | tf_op jit(solution)/shard_map/ppermute | solution.py:329
  34.3 1.4 %shard_map.54.steps_ref = f32[1024,128]{1,0:T(8,128)S(1)} custom-call(f32[5,16,16,128]{3,2,1,0:T(8,128)S(1)} %get-tuple-element.32.held_ref, f32[16,16,128]{2,1,0:T(8,128)S(1)} %collective-permute-done.9.swapped_ref, f32[1024,128]{1,0:T(8,128)S(1)} %bitcast.17, bf16[16,384,256]{2,1,0:T(8,128)(2,1)S(1)} %get-tuple-element.21.fine_ref), custom_call_target="tpu_custom_call" | custom-call | flops 1000000000 | bytes 1000000 | tf_op jit(solution)/shard_map/pallas_call | solution.py:393
  35.7 0.0 collective-permute-done.10.swapped_ref
  35.7 0.9 %shard_map.55 = f32[1024,128]{1,0:T(8,128)} custom-call(f32[1024,128]{1,0:T(8,128)S(1)} %shard_map.54.steps_ref, f32[5,16,16,128]{3,2,1,0:T(8,128)S(1)} %get-tuple-element.32.held_ref, f32[16,16,128]{2,1,0:T(8,128)S(1)} %collective-permute-done.10.swapped_ref), custom_call_target="tpu_custom_call" | custom-call | flops 1000000 | bytes 1000000 | tf_op jit(solution)/shard_map/pallas_call | solution.py:394
  (4 shorter events, 0.0 us)
Async XLA Ops:
  4.6 3.6 %collective-permute-start = (f32[16,16,128]{2,1,0:T(8,128)S(1)}, f32[16,16,128]{2,1,0:T(8,128)S(1)}, u32[]{:S(2)}, u32[]{:S(2)}) collective-permute-start(f32[16,16,128]{2,1,0:T(8,128)S(1)} %get-tuple-element.20), channel_id=1, source_target_pairs={{0,1},{1,2},{2,3},{3,4},{4,5},{5,6},{6,7},{7,8},{8,9},{9,10},{10,1... | collective-permute-start | bytes 393224 | tf_op jit(solution)/shard_map/ppermute | solution.py:329
  6.3 2.0 %copy-start = (f32[2,4,16384]{2,1,0:T(4,128)S(1)}, f32[2,4,16384]{2,1,0:T(4,128)}, u32[]{:S(2)}) copy-start(f32[2,4,16384]{2,1,0:T(4,128)} %param.5) | copy-start | bytes 1572868
  6.3 2.0 %copy-start.1 = (f32[2,16384]{1,0:T(2,128)S(1)}, f32[2,16384]{1,0:T(2,128)}, u32[]{:S(2)}) copy-start(f32[2,16384]{1,0:T(2,128)} %param.4) | copy-start | bytes 393220
  10.4 3.5 %collective-permute-start.3 = (f32[16,16,128]{2,1,0:T(8,128)S(1)}, f32[16,16,128]{2,1,0:T(8,128)S(1)}, u32[]{:S(2)}, u32[]{:S(2)}) collective-permute-start(f32[16,16,128]{2,1,0:T(8,128)S(1)} %shard_map.48.own_ref.refs_0_), channel_id=1, source_target_pairs={{0,12},{1,3},{2,1},{3,2},{4,5},{5,4},{6,7},{7,6},{8,9},{9,8},{10,1... | collective-permute-start | bytes 393224 | tf_op jit(solution)/shard_map/ppermute | solution.py:353
  13.0 1.3 %collective-permute-start.1 = (f32[16,16,128]{2,1,0:T(8,128)S(1)}, f32[16,16,128]{2,1,0:T(8,128)S(1)}, u32[]{:S(2)}, u32[]{:S(2)}) collective-permute-start(f32[16,16,128]{2,1,0:T(8,128)S(1)} %shard_map.48.own_ref.refs_0_), channel_id=1, source_target_pairs={{0,1},{1,0},{2,3},{3,2},{4,5},{5,4},{6,7},{7,6},{8,9},{9,8},{10,11... | collective-permute-start | bytes 393224 | tf_op jit(solution)/shard_map/ppermute | solution.py:329
  13.1 5.1 %collective-permute-start.2 = (f32[16,16,128]{2,1,0:T(8,128)S(1)}, f32[16,16,128]{2,1,0:T(8,128)S(1)}, u32[]{:S(2)}, u32[]{:S(2)}) collective-permute-start(f32[16,16,128]{2,1,0:T(8,128)S(1)} %shard_map.48.own_ref.refs_0_), channel_id=1, source_target_pairs={{0,3},{1,0},{2,1},{3,2},{4,7},{5,4},{6,5},{7,6},{8,11},{9,8},{10,9... | collective-permute-start | bytes 393224 | tf_op jit(solution)/shard_map/ppermute | solution.py:329
  14.3 5.5 %collective-permute-start.4 = (f32[16,16,128]{2,1,0:T(8,128)S(1)}, f32[16,16,128]{2,1,0:T(8,128)S(1)}, u32[]{:S(2)}, u32[]{:S(2)}) collective-permute-start(f32[16,16,128]{2,1,0:T(8,128)S(1)} %shard_map.48.own_ref.refs_0_), channel_id=1, source_target_pairs={{0,2},{1,3},{2,0},{3,1},{4,6},{5,7},{6,4},{7,5},{8,10},{9,11},{10,... | collective-permute-start | bytes 393224 | tf_op jit(solution)/shard_map/ppermute | solution.py:329
  14.4 5.4 %collective-permute-start.6 = (f32[16,16,128]{2,1,0:T(8,128)S(1)}, f32[16,16,128]{2,1,0:T(8,128)S(1)}, u32[]{:S(2)}, u32[]{:S(2)}) collective-permute-start(f32[16,16,128]{2,1,0:T(8,128)S(1)} %get-tuple-element.25), channel_id=1, source_target_pairs={{0,1},{1,2},{2,0},{3,7},{4,5},{5,4},{6,3},{7,6},{8,9},{9,8},{10,11... | collective-permute-start | bytes 393224 | tf_op jit(solution)/shard_map/ppermute | solution.py:377
  15.2 4.6 %collective-permute-start.5 = (f32[16,16,128]{2,1,0:T(8,128)S(1)}, f32[16,16,128]{2,1,0:T(8,128)S(1)}, u32[]{:S(2)}, u32[]{:S(2)}) collective-permute-start(f32[16,16,128]{2,1,0:T(8,128)S(1)} %get-tuple-element.25), channel_id=1, source_target_pairs={{0,1},{1,0},{2,3},{3,5},{4,2},{5,4},{6,10},{7,11},{8,9},{9,8},{10,... | collective-permute-start | bytes 393224 | tf_op jit(solution)/shard_map/ppermute | solution.py:377
  19.8 6.7 %collective-permute-start.7 = (f32[16,16,128]{2,1,0:T(8,128)S(1)}, f32[16,16,128]{2,1,0:T(8,128)S(1)}, u32[]{:S(2)}, u32[]{:S(2)}) collective-permute-start(f32[16,16,128]{2,1,0:T(8,128)S(1)} %get-tuple-element.27), channel_id=1, source_target_pairs={{0,1},{1,0},{2,3},{3,2},{4,6},{5,9},{6,4},{7,11},{8,5},{9,8},{10,7... | collective-permute-start | bytes 393224 | tf_op jit(solution)/shard_map/ppermute | solution.py:349
  28.4 4.5 %collective-permute-start.8 = (f32[16,16,128]{2,1,0:T(8,128)S(1)}, f32[16,16,128]{2,1,0:T(8,128)S(1)}, u32[]{:S(2)}, u32[]{:S(2)}) collective-permute-start(f32[16,16,128]{2,1,0:T(8,128)S(1)} %get-tuple-element.29), channel_id=1, source_target_pairs={{0,1},{1,0},{2,3},{3,2},{4,5},{5,4},{6,7},{7,6},{8,10},{9,13},{10,... | collective-permute-start | bytes 393224 | tf_op jit(solution)/shard_map/ppermute | solution.py:349
  32.9 1.4 %collective-permute-start.9 = (f32[16,16,128]{2,1,0:T(8,128)S(1)}, f32[16,16,128]{2,1,0:T(8,128)S(1)}, u32[]{:S(2)}, u32[]{:S(2)}) collective-permute-start(f32[16,16,128]{2,1,0:T(8,128)S(1)} %get-tuple-element.33), channel_id=1, source_target_pairs={{0,1},{1,0},{2,3},{3,2},{4,5},{5,4},{6,7},{7,6},{8,9},{9,8},{10,11... | collective-permute-start | bytes 393224 | tf_op jit(solution)/shard_map/ppermute | solution.py:329
  33.0 2.7 %collective-permute-start.10 = (f32[16,16,128]{2,1,0:T(8,128)S(1)}, f32[16,16,128]{2,1,0:T(8,128)S(1)}, u32[]{:S(2)}, u32[]{:S(2)}) collective-permute-start(f32[16,16,128]{2,1,0:T(8,128)S(1)} %get-tuple-element.34), channel_id=1, source_target_pairs={{0,1},{1,0},{2,3},{3,2},{4,5},{5,4},{6,7},{7,6},{8,9},{9,8},{10,11... | collective-permute-start | bytes 393224 | tf_op jit(solution)/shard_map/ppermute | solution.py:329
